TPU v7x, 32 devices: a whole 2x2x4 slice. The times are simulated.
32 devices in a mesh: data: 32 (over z, y, x, core).
Axes of the slice: x: 2, y: 2, z: 4, core: 2. Of those that a mesh axis runs over, the one named last changes fastest.
Arguments:
- inputs_now: bfloat16 [32768, 1536], P('data')
- targets_now: bfloat16 [32768, 4096], P('data')
- inputs_next: bfloat16 [32768, 1536], P('data')
- targets_next: bfloat16 [32768, 4096], P('data')
- w_up: float32 [1, 1536, 6144], replicated
- w_down: float32 [1, 6144, 1536], replicated
- w_head: float32 [1536, 4096], replicated
- mom_up: float32 [1, 1536, 6144], replicated
- mom_down: float32 [1, 6144, 1536], replicated
- mom_head: float32 [1536, 4096], replicated
Outputs:
- output 1: float32 [1, 1536, 6144], replicated
- output 2: float32 [1, 6144, 1536], replicated
- output 3: float32 [1536, 4096], replicated
- output 4: float32 [1, 1536, 6144], replicated
- output 5: float32 [1, 6144, 1536], replicated
- output 6: float32 [1536, 4096], replicated
- output 7: float32 [32768], P('data')
- output 8: float32 [32768, 1536], P('data')
All inputs are finite; a program needn't handle non-finite values.
Results may differ from a plain program's by a relative error of at most 0.00580266.
Values are sent between devices in bfloat16 or wider.
A program may use at most 1.75 GiB of HBM per device.

v0:
```python
import jax
import jax.numpy as jnp
from jax import lax
from jax.sharding import PartitionSpec as P

MOMENTUM = 0.9
RATE_BASE = 0.5
ROW_DIMS = (((0,), (0,)), ((), ()))
COL_DIMS = (((1,), (1,)), ((), ()))


def forward_saving(up_bf, down_bf, hidden):
    saved_acts = []
    for layer_idx in range(up_bf.shape[0]):
        hidden_bf = hidden.astype(jnp.bfloat16)
        pre_act = jnp.dot(hidden_bf, up_bf[layer_idx], preferred_element_type=jnp.float32)
        act_f32, gelu_back = jax.vjp(jax.nn.gelu, pre_act)
        act_bf = act_f32.astype(jnp.bfloat16)
        saved_acts.append((hidden_bf, act_bf, gelu_back))
        hidden = hidden + jnp.dot(act_bf, down_bf[layer_idx], preferred_element_type=jnp.float32)
    return hidden.astype(jnp.bfloat16), saved_acts


def layer_backward(saved_layer, up_layer, down_layer, grad_hidden, need_input_grad):
    hidden_bf, act_bf, gelu_back = saved_layer
    grad_hidden_bf = grad_hidden.astype(jnp.bfloat16)
    down_local = lax.dot_general(act_bf, grad_hidden_bf, ROW_DIMS, preferred_element_type=jnp.float32)
    grad_act = lax.dot_general(grad_hidden_bf, down_layer, COL_DIMS, preferred_element_type=jnp.float32)
    grad_pre = gelu_back(grad_act)[0].astype(jnp.bfloat16)
    up_local = lax.dot_general(hidden_bf, grad_pre, ROW_DIMS, preferred_element_type=jnp.float32)
    if need_input_grad:
        grad_hidden = grad_hidden + lax.dot_general(grad_pre, up_layer, COL_DIMS, preferred_element_type=jnp.float32)
    return up_local.astype(jnp.bfloat16), down_local.astype(jnp.bfloat16), grad_hidden


def sgd_update(weight, moment, gradient, learn_rate):
    new_moment = MOMENTUM * moment + gradient.astype(jnp.float32)
    return weight - learn_rate * new_moment, new_moment


def second_step(w_up, w_down, w_head, mom_up, mom_down, mom_head, grad_up, grad_down, grad_head, inputs_next, targets_next):
    learn_rate = RATE_BASE / w_up.shape[0]
    new_up, new_down, new_mom_up, new_mom_down = [], [], [], []
    hidden = inputs_next.astype(jnp.float32)
    for layer_idx in range(w_up.shape[0]):
        up_new, up_moment = sgd_update(w_up[layer_idx], mom_up[layer_idx], grad_up[layer_idx], learn_rate)
        down_new, down_moment = sgd_update(w_down[layer_idx], mom_down[layer_idx], grad_down[layer_idx], learn_rate)
        new_up.append(up_new)
        new_down.append(down_new)
        new_mom_up.append(up_moment)
        new_mom_down.append(down_moment)
        pre_act = jnp.dot(hidden.astype(jnp.bfloat16), up_new.astype(jnp.bfloat16), preferred_element_type=jnp.float32)
        act_bf = jax.nn.gelu(pre_act).astype(jnp.bfloat16)
        hidden = hidden + jnp.dot(act_bf, down_new.astype(jnp.bfloat16), preferred_element_type=jnp.float32)
    head_new, head_moment = sgd_update(w_head, mom_head, grad_head, learn_rate)
    logits = jnp.dot(hidden.astype(jnp.bfloat16), head_new.astype(jnp.bfloat16), preferred_element_type=jnp.float32)
    logit_err = logits - targets_next.astype(jnp.float32)
    errors = jnp.sum(logit_err * logit_err, axis=-1) / (2.0 * w_head.shape[1])
    return (jnp.stack(new_up), jnp.stack(new_down), head_new, jnp.stack(new_mom_up), jnp.stack(new_mom_down), head_moment, errors, hidden)


def solution(mesh):
    data_size = mesh.shape['data']

    def device_step(inputs_now, targets_now, inputs_next, targets_next, w_up, w_down, w_head, mom_up, mom_down, mom_head):
        layers = w_up.shape[0]
        loss_scale = 1.0 / (inputs_now.shape[0] * data_size * w_head.shape[1])
        up_bf = w_up.astype(jnp.bfloat16)
        down_bf = w_down.astype(jnp.bfloat16)
        head_bf = w_head.astype(jnp.bfloat16)
        top_bf, saved_acts = forward_saving(up_bf, down_bf, inputs_now.astype(jnp.float32))
        logits = jnp.dot(top_bf, head_bf, preferred_element_type=jnp.float32)
        grad_logits = ((logits - targets_now.astype(jnp.float32)) * loss_scale).astype(jnp.bfloat16)
        head_local = lax.dot_general(top_bf, grad_logits, ROW_DIMS, preferred_element_type=jnp.float32).astype(jnp.bfloat16)
        grad_head = lax.psum(head_local, 'data')
        grad_hidden = lax.dot_general(grad_logits, head_bf, COL_DIMS, preferred_element_type=jnp.float32)
        grad_up = [None] * layers
        grad_down = [None] * layers
        for layer_idx in reversed(range(layers)):
            up_local, down_local, grad_hidden = layer_backward(saved_acts[layer_idx], up_bf[layer_idx], down_bf[layer_idx], grad_hidden, layer_idx > 0)
            grad_down[layer_idx] = lax.psum(down_local, 'data')
            grad_up[layer_idx] = lax.psum(up_local, 'data')
        return second_step(w_up, w_down, w_head, mom_up, mom_down, mom_head, grad_up, grad_down, grad_head, inputs_next, targets_next)

    row_spec = P('data', None)
    in_specs = (row_spec, row_spec, row_spec, row_spec, P(), P(), P(), P(), P(), P())
    out_specs = (P(), P(), P(), P(), P(), P(), P('data'), row_spec)
    return jax.shard_map(device_step, mesh=mesh, in_specs=in_specs, out_specs=out_specs, check_vma=False)
```

profile of v0, /device:TPU:0, one launch (start us, length us, event | category | flops | bytes accessed | tf_op | source)
XLA Modules:
  0.0 1274.5 jit_solution(12001452589985323008)
XLA Ops:
  7.2 0.0 copy-start
  7.2 0.0 all-reduce.3.cloned.1.call-start
  7.2 33.3 %fusion.22 = f32[1024,6144]{1,0:T(8,128)} fusion(bf16[1024,1536]{1,0:T(8,128)(2,1)} %param.10, f32[1,1536,6144]{2,1,0:T(8,128)} %param.14), kind=kOutput, calls=%fused_computation.34 | convolution fusion | flops 19336790016 | bytes 66060288 | tf_op jit(solution)/shard_map/dot_general | solution.py:16
  40.5 0.0 copy-done
  40.5 29.9 %add_convert_fusion = bf16[1024,1536]{1,0:T(8,128)(2,1)} fusion(bf16[1024,1536]{1,0:T(8,128)(2,1)S(1)} %copy-done, f32[1,6144,1536]{2,1,0:T(8,128)} %param.15, f32[1024,6144]{1,0:T(8,128)} %fusion.22), kind=kOutput, calls=%fused_computation.52 | convolution fusion | flops 19398131712 | bytes 69206016 | tf_op jit(solution)/shard_map/dot_general | solution.py:20
  70.4 22.5 %multiply_convert_fusion.1 = bf16[1024,4096]{1,0:T(8,128)(2,1)} fusion(bf16[1024,4096]{1,0:T(8,128)(2,1)} %param.11, bf16[1024,1536]{1,0:T(8,128)(2,1)} %add_convert_fusion, f32[1536,4096]{1,0:T(8,128)} %param.16), kind=kOutput, calls=%fused_computation.42 | convolution fusion | flops 12907970560 | bytes 45088768 | tf_op jit(solution)/shard_map/dot_general | solution.py:72
  93.0 0.0 copy-start.3
  93.0 21.6 %fusion.49 = bf16[1024,1536]{1,0:T(8,128)(2,1)} fusion(bf16[1024,4096]{1,0:T(8,128)(2,1)} %multiply_convert_fusion.1, f32[1536,4096]{1,0:T(8,128)} %param.16), kind=kOutput, calls=%fused_computation.53 | convolution fusion | flops 12892766208 | bytes 36700160 | tf_op jit(solution)/shard_map/dot_general | solution.py:76
  114.6 0.0 copy-done.3
  114.6 0.0 copy-start.4
  114.6 19.4 %convolution_convert_fusion.2 = bf16[1536,4096]{1,0:T(8,128)(2,1)} fusion(bf16[1024,1536]{1,0:T(8,128)(2,1)S(1)} %copy-done.3, bf16[1024,4096]{1,0:T(8,128)(2,1)} %multiply_convert_fusion.1), kind=kOutput, calls=%fused_computation.43 | convolution fusion | flops 12891193344 | bytes 24117248 | tf_op jit(solution)/shard_map/dot_general | solution.py:74
  134.0 0.0 copy-done.4
  134.0 0.0 copy-start.1
  134.1 30.3 %convolution_convert_fusion = bf16[6144,1536]{1,0:T(8,128)(2,1)} fusion(bf16[1024,1536]{1,0:T(8,128)(2,1)S(1)} %copy-done.4, f32[1024,6144]{1,0:T(8,128)} %fusion.22), kind=kOutput, calls=%fused_computation.27 | convolution fusion | flops 19393413120 | bytes 47185920 | tf_op jit(solution)/shard_map/dot_general | solution.py:27
  164.3 0.0 copy-done.1
  164.3 54.7 %fusion.17 = bf16[1536,6144]{0,1:T(8,128)(2,1)} fusion(bf16[1024,1536]{1,0:T(8,128)(2,1)S(1)} %copy-done.1, f32[1024,6144]{1,0:T(8,128)} %fusion.22, bf16[1024,1536]{1,0:T(8,128)(2,1)} %fusion.49, f32[1,6144,1536]{2,1,0:T(8,128)} %param.15), kind=kOutput, calls=%fused_computation.29 | convolution fusion | flops 38799409152 | bytes 88080384 | tf_op jit(solution)/shard_map/dot_general | solution.py:30
  219.1 0.0 all-reduce.3.cloned.1.call-update
  219.1 36.8 %copy.18 = f32[1,1536,6144]{1,2,0:T(8,128)} copy(f32[1,1536,6144]{2,1,0:T(8,128)} %param.14) | data formatting | bytes 75497472 | tf_op args[4]
  255.8 36.8 %copy.19 = f32[1,1536,6144]{1,2,0:T(8,128)} copy(f32[1,1536,6144]{2,1,0:T(8,128)} %param.17) | data formatting | bytes 75497472 | tf_op args[7]
  292.6 651.0 %all-reduce.3.cloned.1.call-done = (bf16[1536,6144]{0,1:T(8,128)(2,1)}, bf16[6144,1536]{1,0:T(8,128)(2,1)}, bf16[1536,4096]{1,0:T(8,128)(2,1)}) async-done(((bf16[1536,6144]{0,1:T(8,128)(2,1)}, bf16[6144,1536]{1,0:T(8,128)(2,1)}, bf16[1536,4096]{1,0:T(8,128)(2,1)}), (bf16[1536,6144]{0,1:T(8,128)(2,1)}, bf16[6144,1536]{1,0:T(8,128)(2,1)}, bf16[1536,4096]{1,0:T(8,128)(2,1)})) %all-reduce.3.cloned.1.call-update) | async-done | bytes 50331664 | tf_op jit(solution)/shard_map/psum | solution.py:82
  943.6 0.0 copy-start.2
  943.6 56.8 %fusion.15 = (f32[1,1536,6144]{1,2,0:T(8,128)}, f32[1,1536,6144]{1,2,0:T(8,128)}) fusion(bf16[1536,6144]{0,1:T(8,128)(2,1)} %get-tuple-element.16, f32[1,1536,6144]{1,2,0:T(8,128)} %copy.19, f32[1,1536,6144]{1,2,0:T(8,128)} %copy.18), kind=kLoop, calls=%fused_computation.25 | loop fusion | flops 47185920 | bytes 169869312 | tf_op jit(solution)/shard_map/stack | solution.py:59
  1000.4 0.0 copy-done.2
  1000.4 39.3 %fusion.14.clone.5 = bf16[1024,6144]{1,0:T(8,128)(2,1)} fusion(bf16[1024,1536]{1,0:T(8,128)(2,1)S(1)} %copy-done.2, f32[1,1536,6144]{1,2,0:T(8,128)} %copy.18, bf16[1536,6144]{0,1:T(8,128)(2,1)} %get-tuple-element.16, f32[1,1536,6144]{1,2,0:T(8,128)} %copy.19), kind=kOutput, calls=%fused_computation.21.clone.clone.clone.2 | convolution fusion | flops 19440599040 | bytes 110100480 | tf_op jit(solution)/shard_map/dot_general | solution.py:52
  1039.7 56.5 %fusion.16 = (f32[1,6144,1536]{2,1,0:T(8,128)}, f32[1,6144,1536]{2,1,0:T(8,128)}) fusion(bf16[6144,1536]{1,0:T(8,128)(2,1)} %get-tuple-element.17, f32[1,6144,1536]{2,1,0:T(8,128)} %param.18, f32[1,6144,1536]{2,1,0:T(8,128)} %param.15), kind=kLoop, calls=%fused_computation.26 | loop fusion | flops 47185920 | bytes 169869312 | tf_op jit(solution)/shard_map/stack | solution.py:59
  1096.2 39.7 %convert_add_fusion.1 = f32[1024,1536]{1,0:T(8,128)} fusion(bf16[1024,1536]{1,0:T(8,128)(2,1)S(1)} %copy-done.2, f32[1,6144,1536]{2,1,0:T(8,128)} %param.15, bf16[6144,1536]{1,0:T(8,128)(2,1)} %get-tuple-element.17, f32[1,6144,1536]{2,1,0:T(8,128)} %param.18, bf16[1024,6144]{1,0:T(8,128)(2,1)} %fusion.14.clone.5), kind=kOutput, calls=%fused_computation.48 | convolution fusion | flops 19387121664 | bytes 116391936 | tf_op jit(solution)/shard_map/dot_general | solution.py:54
  1136.0 36.8 %copy.22 = f32[1,1536,6144]{2,1,0:T(8,128)} copy(f32[1,1536,6144]{1,2,0:T(8,128)} %get-tuple-element.23) | data formatting | bytes 75497472
  1172.7 36.8 %copy.21 = f32[1,1536,6144]{2,1,0:T(8,128)} copy(f32[1,1536,6144]{1,2,0:T(8,128)} %get-tuple-element.24) | data formatting | bytes 75497472
  1209.5 35.6 %multiply_subtract_fusion = (f32[1536,4096]{1,0:T(8,128)}, f32[1536,4096]{1,0:T(8,128)}) fusion(f32[1536,4096]{1,0:T(8,128)} %param.16, bf16[1536,4096]{1,0:T(8,128)(2,1)} %get-tuple-element.18, f32[1536,4096]{1,0:T(8,128)} %param.19), kind=kLoop, calls=%fused_computation.22 | loop fusion | flops 31457280 | bytes 113246208 | tf_op jit(solution)/shard_map/sub | solution.py:38
  1245.1 21.8 %multiply_reduce_fusion = f32[1024]{0:T(1024)S(1)} fusion(bf16[1024,4096]{1,0:T(8,128)(2,1)} %param.13, f32[1536,4096]{1,0:T(8,128)} %get-tuple-element.19, f32[1024,1536]{1,0:T(8,128)} %convert_add_fusion.1), kind=kOutput, calls=%fused_computation.41 | convolution fusion | flops 12909542400 | bytes 39849984 | tf_op jit(solution)/shard_map/dot_general | solution.py:56
  1267.0 0.6 broadcast_multiply_fusion
Async XLA Ops:
  7.2 33.3 %copy-start = (bf16[1024,1536]{1,0:T(8,128)(2,1)S(1)}, bf16[1024,1536]{1,0:T(8,128)(2,1)}, u32[]{:S(2)}) copy-start(bf16[1024,1536]{1,0:T(8,128)(2,1)} %param.10) | copy-start | bytes 9437188
  7.2 936.4 %all-reduce.3.cloned.1.call-start = ((), (), s32[]{:S(2)}) async-start(), calls=%async_computation | async-start | bytes 100663296 | tf_op jit(solution)/shard_map/psum | solution.py:82
  93.0 21.6 %copy-start.3 = (bf16[1024,1536]{1,0:T(8,128)(2,1)S(1)}, bf16[1024,1536]{1,0:T(8,128)(2,1)}, u32[]{:S(2)}) copy-start(bf16[1024,1536]{1,0:T(8,128)(2,1)} %add_convert_fusion) | copy-start | bytes 9437188
  114.6 19.4 %copy-start.4 = (bf16[1024,1536]{1,0:T(8,128)(2,1)S(1)}, bf16[1024,1536]{1,0:T(8,128)(2,1)}, u32[]{:S(2)}) copy-start(bf16[1024,1536]{1,0:T(8,128)(2,1)} %fusion.49) | copy-start | bytes 9437188
  134.0 30.3 %copy-start.1 = (bf16[1024,1536]{1,0:T(8,128)(2,1)S(1)}, bf16[1024,1536]{1,0:T(8,128)(2,1)}, u32[]{:S(2)}) copy-start(bf16[1024,1536]{1,0:T(8,128)(2,1)} %param.10) | copy-start | bytes 9437188
  943.6 56.8 %copy-start.2 = (bf16[1024,1536]{1,0:T(8,128)(2,1)S(1)}, bf16[1024,1536]{1,0:T(8,128)(2,1)}, u32[]{:S(2)}) copy-start(bf16[1024,1536]{1,0:T(8,128)(2,1)} %param.12) | copy-start | bytes 9437188
Sparse Core Ops, SparseCore 0:
  219.2 724.3 all-reduce.2
where the time goes:
time: 1280 us; the launch traced here: 1270 us
  waiting for transfers between devices  651 us (51%)
  matrix products  313 us (24%)
  other arithmetic  149 us (12%)
  local copies, waits for them, and re-layouts  147 us (11%)
  between operations  14.2 us (1%)
    psum x1, waiting for transfers between devices, device_step(): grad_up[layer_idx] = lax.psum(up_local, 'data')  651 us
    unnamed x14, local copies, waits for them, and re-layouts  147 us
    another operation x1, other arithmetic, second_step(): jnp.stack(new_mom_up)  56.8 us
    another operation x1, other arithmetic, second_step(): jnp.stack(new_mom_down)  56.5 us
    dot_general x1, matrix products, layer_backward(): lax.dot_general(hidden_bf, grad_pre, ROW_DIMS, preferred_element_type=jnp...  54.7 us
    dot_general x1, matrix products, second_step(): jnp.dot(act_bf, down_new.astype(jnp.bfloat16), preferred_element_type=jnp...  39.7 us
    dot_general x1, matrix products, second_step(): jnp.dot(hidden.astype(jnp.bfloat16), up_new.astype(jnp.bfloat16), preferr...  39.3 us
    sub x1, other arithmetic, sgd_update(): return (weight - learn_rate * new_moment, new_moment)  35.6 us
  transfers between devices with their start and end apart: 1, of which 1 were waited for; matrix products, arithmetic and copies ran while one was open for 6% of the time, Pallas kernels for 0%

commit v1 on v0

v1 whole, which is shorter than its diff:
```python
import functools

import jax
import jax.numpy as jnp
from jax import lax
from jax.experimental import pallas as pl
from jax.experimental.pallas import tpu as pltpu
from jax.sharding import PartitionSpec as P

MOMENTUM = 0.9
RATE_BASE = 0.5
ROW_DIMS = (((0,), (0,)), ((), ()))
COL_DIMS = (((1,), (1,)), ((), ()))
MESH = pl.DeviceIdType.MESH

CORE, X, Y, Z_LOW, Z_HIGH = 1, 2, 4, 8, 16
CHUNK = 512
ACC_SLOTS, RX_SLOTS, SUM_SLOTS = 6, 4, 8
LEVELS = 4


def bit_of(me, stride):
    return lax.rem(lax.div(me, stride), 2)


def partner_of(me, stride):
    return me + stride * (1 - 2 * bit_of(me, stride))


class Part:
    def __init__(self, me, axis_chunk, order, axes, src, out, acc, rx, total, send_sem, recv_sem, load_sem, store_sem):
        self.me, self.axis_chunk, self.order = me, axis_chunk, order
        self.src, self.out, self.acc, self.rx, self.total = src, out, acc, rx, total
        self.send_sem, self.recv_sem, self.load_sem, self.store_sem = send_sem, recv_sem, load_sem, store_sem
        self.chunks = src.shape[axis_chunk] // CHUNK
        nr, nc = acc.shape[1], acc.shape[2]
        self.keep, self.send = [(0, 0, nr, nc)], [None]
        for level in range(1, LEVELS + 1):
            r0, c0, nr, nc = self.keep[-1]
            bit = bit_of(me, order[level])
            if axes[level] == 0:
                nr //= 2
                self.keep.append((pl.multiple_of(r0 + bit * nr, 16), c0, nr, nc))
                self.send.append((pl.multiple_of(r0 + (1 - bit) * nr, 16), c0, nr, nc))
            else:
                nc //= 2
                self.keep.append((r0, pl.multiple_of(c0 + bit * nc, 128), nr, nc))
                self.send.append((r0, pl.multiple_of(c0 + (1 - bit) * nc, 128), nr, nc))

    def half(self, ref, chunk, which):
        size = CHUNK // 2
        start = pl.multiple_of(chunk * CHUNK + which * size, size)
        if self.axis_chunk == 0:
            return ref.at[pl.ds(start, size), :]
        return ref.at[:, pl.ds(start, size)]

    @staticmethod
    def at(ref, slot, region):
        r0, c0, nr, nc = region
        return ref.at[slot, pl.ds(r0, nr), pl.ds(c0, nc)]

    def copy(self, phase, chunk):
        me = self.me
        acc_slot, rx_slot, sum_slot = lax.rem(chunk, ACC_SLOTS), lax.rem(chunk, RX_SLOTS), lax.rem(chunk, SUM_SLOTS)
        core = bit_of(me, CORE)
        if phase == 0:
            source, target = self.half(self.src, chunk, 1 - core), self.rx[0].at[rx_slot]
        elif phase <= LEVELS:
            source, target = self.at(self.acc, acc_slot, self.send[phase]), self.rx[phase].at[rx_slot]
        elif phase <= 2 * LEVELS:
            source = self.at(self.total, sum_slot, self.keep[2 * LEVELS + 1 - phase])
            target = source
        else:
            source, target = self.total.at[sum_slot], self.half(self.out, chunk, core)
        level = phase if phase <= LEVELS else 2 * LEVELS + 1 - phase
        return pltpu.make_async_remote_copy(
            src_ref=source,
            dst_ref=target,
            send_sem=self.send_sem.at[phase, rx_slot],
            recv_sem=self.recv_sem.at[phase, rx_slot],
            device_id=(partner_of(me, self.order[level]),),
            device_id_type=MESH,
        )

    def load(self, chunk):
        slot = lax.rem(chunk, ACC_SLOTS)
        return pltpu.make_async_copy(self.half(self.src, chunk, bit_of(self.me, CORE)), self.acc.at[slot], self.load_sem.at[slot])

    def store(self, chunk):
        slot = lax.rem(chunk, SUM_SLOTS)
        return pltpu.make_async_copy(self.total.at[slot], self.half(self.out, chunk, bit_of(self.me, CORE)), self.store_sem.at[slot])

    def add(self, chunk, level, region, parent, target, target_slot):
        acc_slot, rx_slot = lax.rem(chunk, ACC_SLOTS), lax.rem(chunk, RX_SLOTS)
        r0, c0, nr, nc = region
        rel_r, rel_c = r0 - parent[0], c0 - parent[1]
        rows = max(16, min(nr, 24576 // nc))
        rx = self.rx[level]

        def body(i, carry):
            at_r = pl.multiple_of(r0 + i * rows, 16)
            from_r = pl.multiple_of(rel_r + i * rows, 16)
            to_c = c0 if isinstance(c0, int) else pl.multiple_of(c0, 128)
            from_c = rel_c if isinstance(rel_c, int) else pl.multiple_of(rel_c, 128)
            mine = self.acc[acc_slot, pl.ds(at_r, rows), pl.ds(to_c, nc)].astype(jnp.float32)
            theirs = rx[rx_slot, pl.ds(from_r, rows), pl.ds(from_c, nc)].astype(jnp.float32)
            target[target_slot, pl.ds(at_r, rows), pl.ds(to_c, nc)] = (mine + theirs).astype(jnp.bfloat16)
            return carry

        lax.fori_loop(0, nr // rows, body, 0)

    def stage(self, number, chunk):
        if number == 0:
            self.load(chunk).start()
            self.copy(0, chunk).start()
            return
        if number == 1:
            self.load(chunk).wait()
        self.copy(number - 1, chunk).wait()
        if number <= LEVELS:
            slot = lax.rem(chunk, ACC_SLOTS)
            parent = self.keep[number - 1]
            self.add(chunk, number - 1, self.send[number], parent, self.acc, slot)
            self.copy(number, chunk).start()
            self.add(chunk, number - 1, self.keep[number], parent, self.acc, slot)
        elif number == LEVELS + 1:
            last = self.keep[LEVELS]
            self.add(chunk, LEVELS, last, last, self.total, lax.rem(chunk, SUM_SLOTS))
            self.copy(number, chunk).start()
        elif number <= 2 * LEVELS:
            self.copy(number, chunk).start()
        elif number == 2 * LEVELS + 1:
            self.copy(number, chunk).start()
            self.store(chunk).start()
        else:
            self.store(chunk).wait()


PART_REFS = 2 + LEVELS + 1 + 4


def sum_kernel(up_ref, down_ref, up_out, down_out, *scratch):
    me = lax.axis_index('data')
    strides = (CORE, X, Y, Z_LOW, Z_HIGH)
    barrier = pltpu.get_barrier_semaphore()
    for stride in strides:
        pl.semaphore_signal(barrier, inc=1, device_id=(partner_of(me, stride),), device_id_type=MESH)
    pl.semaphore_wait(barrier, len(strides))

    def build(axis_chunk, order, axes, src, out, refs):
        acc, rx, total = refs[0], refs[1:2 + LEVELS], refs[2 + LEVELS]
        return Part(me, axis_chunk, order, axes, src, out, acc, rx, total, *refs[3 + LEVELS:])

    parts = (
        build(1, (CORE, X, Z_LOW, Y, Z_HIGH), (1, 1, 0, 0, 0), up_ref, up_out, scratch[:PART_REFS]),
        build(0, (CORE, Y, Z_LOW, X, Z_HIGH), (0, 0, 0, 0, 0), down_ref, down_out, scratch[PART_REFS:]),
    )
    stages = 2 * LEVELS + 3

    def tick(t, carry):
        for number in range(stages):
            for part in parts:
                chunk = t - number

                @pl.when(jnp.logical_and(chunk >= 0, chunk < part.chunks))
                def _():
                    part.stage(number, chunk)
        return carry

    lax.fori_loop(0, max(part.chunks for part in parts) + stages - 1, tick, 0)


def part_scratch(rows, cols, axes):
    shapes = [pltpu.VMEM((ACC_SLOTS, rows, cols), jnp.bfloat16), pltpu.VMEM((RX_SLOTS, rows, cols), jnp.bfloat16)]
    nr, nc = rows, cols
    for level in range(1, LEVELS + 1):
        nr, nc = (nr // 2, nc) if axes[level] == 0 else (nr, nc // 2)
        shapes.append(pltpu.VMEM((RX_SLOTS, nr, nc), jnp.bfloat16))
    shapes.append(pltpu.VMEM((SUM_SLOTS, rows, cols), jnp.bfloat16))
    phases = 2 * LEVELS + 2
    shapes += [pltpu.SemaphoreType.DMA((phases, RX_SLOTS)), pltpu.SemaphoreType.DMA((phases, RX_SLOTS))]
    shapes += [pltpu.SemaphoreType.DMA((ACC_SLOTS,)), pltpu.SemaphoreType.DMA((SUM_SLOTS,))]
    return shapes


def sum_gradients(up_local, down_local):
    scratch = part_scratch(up_local.shape[0], CHUNK // 2, (1, 1, 0, 0, 0))
    scratch += part_scratch(CHUNK // 2, down_local.shape[1], (0, 0, 0, 0, 0))
    any_spec = pl.BlockSpec(memory_space=pl.ANY)
    size = up_local.size + down_local.size
    return pl.pallas_call(
        sum_kernel,
        out_shape=[jax.ShapeDtypeStruct(up_local.shape, jnp.bfloat16), jax.ShapeDtypeStruct(down_local.shape, jnp.bfloat16)],
        in_specs=[any_spec] * 2,
        out_specs=[any_spec] * 2,
        scratch_shapes=scratch,
        compiler_params=pltpu.CompilerParams(collective_id=0, has_side_effects=True, vmem_limit_bytes=60 * 2**20),
        cost_estimate=pl.CostEstimate(flops=280 * 10**9, bytes_accessed=8 * size, transcendentals=0),
        name='sum_gradients',
    )(up_local, down_local)


def update(weight_ref, moment_ref, grad_ref, weight_out, moment_out, rate):
    new_moment = MOMENTUM * moment_ref[...] + grad_ref[...].astype(jnp.float32)
    new_weight = weight_ref[...] - rate * new_moment
    moment_out[...] = new_moment
    weight_out[...] = new_weight
    return new_weight.astype(jnp.bfloat16)


def up_kernel(rate, rows_ref, weight_ref, moment_ref, grad_ref, weight_out, moment_out, act_out):
    weight_bf = update(weight_ref, moment_ref, grad_ref, weight_out, moment_out, rate)
    pre_act = jnp.dot(rows_ref[...], weight_bf, preferred_element_type=jnp.float32)
    act_out[...] = jax.nn.gelu(pre_act).astype(jnp.bfloat16)


def down_kernel(rate, rows_ref, act_ref, weight_ref, moment_ref, grad_ref, weight_out, moment_out, hidden_out, hidden_bf_out):
    step = pl.program_id(0)
    weight_bf = update(weight_ref, moment_ref, grad_ref, weight_out, moment_out, rate)

    @pl.when(step == 0)
    def _():
        hidden_out[...] = rows_ref[...].astype(jnp.float32)

    hidden_out[...] += jnp.dot(act_ref[...], weight_bf, preferred_element_type=jnp.float32)

    @pl.when(step == pl.num_programs(0) - 1)
    def _():
        hidden_bf_out[...] = hidden_out[...].astype(jnp.bfloat16)


def head_kernel(rate, hidden_ref, target_ref, weight_ref, moment_ref, grad_ref, weight_out, moment_out, error_out):
    weight_bf = update(weight_ref, moment_ref, grad_ref, weight_out, moment_out, rate)
    logits = jnp.dot(hidden_ref[...], weight_bf, preferred_element_type=jnp.float32)
    logit_err = logits - target_ref[...].astype(jnp.float32)
    squares = logit_err * logit_err
    folded = squares[:, :128]
    for start in range(128, squares.shape[1], 128):
        folded += squares[:, start:start + 128]

    @pl.when(pl.program_id(0) == 0)
    def _():
        error_out[...] = jnp.zeros_like(error_out)

    error_out[...] += folded


def whole(shape):
    return pl.BlockSpec(shape, lambda i: (0, 0))


def step_call(kernel, rate, steps, in_specs, out_specs, out_shape, flops, name, args):
    return pl.pallas_call(
        functools.partial(kernel, rate),
        grid=(steps,),
        in_specs=in_specs,
        out_specs=out_specs,
        out_shape=out_shape,
        compiler_params=pltpu.CompilerParams(dimension_semantics=('arbitrary',), vmem_limit_bytes=60 * 2**20),
        cost_estimate=pl.CostEstimate(flops=flops, bytes_accessed=16 * args[-1].size, transcendentals=0),
        name=name,
    )(*args)


def second_up(rows, weight, moment, grad, rate, tile=256):
    tokens, (model, width) = rows.shape[0], weight.shape
    cols = pl.BlockSpec((model, tile), lambda i: (0, i))
    return step_call(
        up_kernel, rate, width // tile,
        [whole(rows.shape), cols, cols, cols],
        [cols, cols, pl.BlockSpec((tokens, tile), lambda i: (0, i))],
        [jax.ShapeDtypeStruct(weight.shape, jnp.float32)] * 2 + [jax.ShapeDtypeStruct((tokens, width), jnp.bfloat16)],
        2 * tokens * model * width, 'second_up', (rows, weight, moment, grad))


def second_down(rows, act, weight, moment, grad, rate, tile=256):
    tokens, (width, model) = rows.shape[0], weight.shape
    band = pl.BlockSpec((tile, model), lambda i: (i, 0))
    return step_call(
        down_kernel, rate, width // tile,
        [whole(rows.shape), pl.BlockSpec((tokens, tile), lambda i: (0, i)), band, band, band],
        [band, band, whole(rows.shape), whole(rows.shape)],
        [jax.ShapeDtypeStruct(weight.shape, jnp.float32)] * 2 + [jax.ShapeDtypeStruct(rows.shape, jnp.float32), jax.ShapeDtypeStruct(rows.shape, jnp.bfloat16)],
        2 * tokens * model * width, 'second_down', (rows, act, weight, moment, grad))


def second_head(hidden_bf, targets, weight, moment, grad, rate, tile=256):
    tokens, (model, width) = hidden_bf.shape[0], weight.shape
    cols = pl.BlockSpec((model, tile), lambda i: (0, i))
    return step_call(
        head_kernel, rate, width // tile,
        [whole(hidden_bf.shape), pl.BlockSpec((tokens, tile), lambda i: (0, i)), cols, cols, cols],
        [cols, cols, whole((tokens, 128))],
        [jax.ShapeDtypeStruct(weight.shape, jnp.float32)] * 2 + [jax.ShapeDtypeStruct((tokens, 128), jnp.float32)],
        2 * tokens * model * width, 'second_head', (hidden_bf, targets, weight, moment, grad))


def solution(mesh):
    data_size = mesh.shape['data']

    def device_step(inputs_now, targets_now, inputs_next, targets_next, w_up, w_down, w_head, mom_up, mom_down, mom_head):
        rate = RATE_BASE / w_up.shape[0]
        loss_scale = 1.0 / (inputs_now.shape[0] * data_size * w_head.shape[1])
        up, down, up_moment, down_moment = w_up[0], w_down[0], mom_up[0], mom_down[0]
        up_bf, down_bf, head_bf = up.astype(jnp.bfloat16), down.astype(jnp.bfloat16), w_head.astype(jnp.bfloat16)

        pre_act = jnp.dot(inputs_now, up_bf, preferred_element_type=jnp.float32)
        act_f32, gelu_back = jax.vjp(jax.nn.gelu, pre_act)
        act_bf = act_f32.astype(jnp.bfloat16)
        hidden = inputs_now.astype(jnp.float32) + jnp.dot(act_bf, down_bf, preferred_element_type=jnp.float32)
        top_bf = hidden.astype(jnp.bfloat16)
        logits = jnp.dot(top_bf, head_bf, preferred_element_type=jnp.float32)
        grad_logits = ((logits - targets_now.astype(jnp.float32)) * loss_scale).astype(jnp.bfloat16)

        head_local = lax.dot_general(top_bf, grad_logits, ROW_DIMS, preferred_element_type=jnp.float32).astype(jnp.bfloat16)
        grad_head = lax.psum(head_local, 'data')
        grad_hidden = lax.dot_general(grad_logits, head_bf, COL_DIMS, preferred_element_type=jnp.float32)
        grad_hidden_bf = grad_hidden.astype(jnp.bfloat16)
        down_local = lax.dot_general(act_bf, grad_hidden_bf, ROW_DIMS, preferred_element_type=jnp.float32).astype(jnp.bfloat16)
        grad_act = lax.dot_general(grad_hidden_bf, down_bf, COL_DIMS, preferred_element_type=jnp.float32)
        grad_pre = gelu_back(grad_act)[0].astype(jnp.bfloat16)
        up_local = lax.dot_general(inputs_now, grad_pre, ROW_DIMS, preferred_element_type=jnp.float32).astype(jnp.bfloat16)
        grad_up, grad_down = sum_gradients(up_local, down_local)

        up_new, up_moment_new, act_next = second_up(inputs_next, up, up_moment, grad_up, rate)
        down_new, down_moment_new, hidden_next, hidden_next_bf = second_down(inputs_next, act_next, down, down_moment, grad_down, rate)
        head_new, head_moment_new, squares = second_head(hidden_next_bf, targets_next, w_head, mom_head, grad_head, rate)
        errors = jnp.sum(squares, axis=-1) / (2.0 * w_head.shape[1])
        return (up_new[None], down_new[None], head_new, up_moment_new[None], down_moment_new[None], head_moment_new, errors, hidden_next)

    row_spec = P('data', None)
    whole3, whole2 = P(None, None, None), P(None, None)
    in_specs = (row_spec, row_spec, row_spec, row_spec, whole3, whole3, whole2, whole3, whole3, whole2)
    out_specs = (whole3, whole3, whole2, whole3, whole3, whole2, P('data'), row_spec)
    return jax.shard_map(device_step, mesh=mesh, in_specs=in_specs, out_specs=out_specs, check_vma=False)
```

time: 1280 us -> 793 us (0.62)
  waiting for transfers between devices: 651 us -> 0.04 us
  Pallas kernels: 0 us -> 556 us
  other arithmetic: 149 us -> 1.84 us
  local copies, waits for them, and re-layouts: 147 us -> 0.01 us
  matrix products: 313 us -> 214 us
    psum x1, waiting for transfers between devices: 651 us -> 0.02 us  [device_step(): grad_head = lax.psum(head_local, 'data')]
    pallas_call x0 -> x4, Pallas kernels: none -> 556 us  [the longest x1 367 us: sum_gradients(): pl.pallas_call(sum_kernel, out_shape=[jax.ShapeDtypeStruct(up_local.shape...]
    unnamed x14 -> x6, local copies, waits for them, and re-layouts: 147 us -> 0.01 us
    another operation x2 -> x0, other arithmetic: 113 us -> none  [the longest x1 56.8 us: second_step(): jnp.stack(new_mom_up)]
    dot_general x7 -> x4, matrix products: 249 us -> 147 us  [the longest x1 52.1 us: device_step(): lax.dot_general(inputs_now, grad_pre, ROW_DIMS, preferred_element_type=jn...]
    sub x1 -> x0, other arithmetic: 35.6 us -> none  [sgd_update(): return (weight - learn_rate * new_moment, new_moment)]
  transfers between devices with their start and end apart: 1 -> 1, of which waited for: 1 -> 0; matrix products, arithmetic and copies ran while one was open for 6% -> 13% of each run, Pallas kernels for 0% -> 65%
where the time goes in v1:
time: 793 us; the launch traced here: 787 us
  Pallas kernels  556 us (70%)
  matrix products  214 us (27%)
  between operations  14.6 us (2%)
    pallas_call x1, Pallas kernels, sum_gradients(): pl.pallas_call(sum_kernel, out_shape=[jax.ShapeDtypeStruct(up_local.shape...  367 us
    pallas_call x3, Pallas kernels, step_call(): pl.pallas_call(functools.partial(kernel, rate), grid=(steps,), in_specs=i...  189 us
    dot_general x1, matrix products, device_step(): lax.dot_general(inputs_now, grad_pre, ROW_DIMS, preferred_element_type=jn...  52.1 us
    dot_general x1, matrix products, device_step(): pre_act = jnp.dot(inputs_now, up_bf, preferred_element_type=jnp.float32)  33.2 us
    dot_general x1, matrix products, device_step(): lax.dot_general(act_bf, grad_hidden_bf, ROW_DIMS, preferred_element_type=...  31.4 us
    dot_general x1, matrix products, device_step(): jnp.dot(act_bf, down_bf, preferred_element_type=jnp.float32)  30.1 us
    dot_general x1, matrix products, device_step(): logits = jnp.dot(top_bf, head_bf, preferred_element_type=jnp.float32)  26.7 us
    dot_general x1, matrix products, device_step(): lax.dot_general(grad_logits, head_bf, COL_DIMS, preferred_element_type=jn...  21.7 us
  transfers between devices with their start and end apart: 1, of which 0 were waited for; matrix products, arithmetic and copies ran while one was open for 13% of the time, Pallas kernels for 65%

profile of v1, /device:TPU:0, one launch (start us, length us, event | category | flops | bytes accessed | tf_op | source)
XLA Modules:
  0.0 786.7 jit_solution(12789536690147820874)
XLA Ops:
  7.2 0.0 copy-start
  7.2 0.0 all-reduce.2.cloned.1.call-start
  7.2 33.2 %fusion.42 = f32[1024,6144]{1,0:T(8,128)} fusion(bf16[1024,1536]{1,0:T(8,128)(2,1)} %param.10, f32[1,1536,6144]{2,1,0:T(8,128)} %param.14), kind=kOutput, calls=%fused_computation.37 | convolution fusion | flops 19327352832 | bytes 66060288 | tf_op jit(solution)/shard_map/dot_general | solution.py:307
  40.4 0.0 copy-done
  40.4 30.1 %add_convert_fusion = bf16[1024,1536]{1,0:T(8,128)(2,1)} fusion(bf16[1024,1536]{1,0:T(8,128)(2,1)S(1)} %copy-done, f32[1024,6144]{1,0:T(8,128)} %fusion.42, f32[1,6144,1536]{2,1,0:T(8,128)} %param.15), kind=kOutput, calls=%fused_computation.24 | convolution fusion | flops 19388694528 | bytes 69206016 | tf_op jit(solution)/shard_map/dot_general | solution.py:310
  70.5 0.0 copy-start.2
  70.5 26.7 %multiply_convert_fusion.1 = bf16[1024,4096]{1,0:T(8,128)(2,1)} fusion(bf16[1024,4096]{1,0:T(8,128)(2,1)} %param.11, bf16[1024,1536]{1,0:T(8,128)(2,1)} %add_convert_fusion, f32[1536,4096]{1,0:T(8,128)} %weight_ref.1), kind=kOutput, calls=%fused_computation.15 | convolution fusion | flops 12907970560 | bytes 45088768 | tf_op jit(solution)/shard_map/dot_general | solution.py:312
  97.2 0.0 copy-done.2
  97.2 19.0 %convolution_convert_fusion.2 = bf16[1536,4096]{1,0:T(8,128)(2,1)} fusion(bf16[1024,1536]{1,0:T(8,128)(2,1)S(1)} %copy-done.2, bf16[1024,4096]{1,0:T(8,128)(2,1)} %multiply_convert_fusion.1), kind=kOutput, calls=%fused_computation.16 | convolution fusion | flops 12891193344 | bytes 24117248 | tf_op jit(solution)/shard_map/dot_general | solution.py:315
  116.3 0.0 all-reduce.2.cloned.1.call-update
  116.3 21.7 %fusion.24 = bf16[1024,1536]{1,0:T(8,128)(2,1)} fusion(bf16[1024,4096]{1,0:T(8,128)(2,1)} %multiply_convert_fusion.1, f32[1536,4096]{1,0:T(8,128)} %weight_ref.1), kind=kOutput, calls=%fused_computation.25 | convolution fusion | flops 12892766208 | bytes 36700160 | tf_op jit(solution)/shard_map/dot_general | solution.py:317
  138.0 0.0 copy-start.1
  138.0 31.4 %convolution_convert_fusion.down_ref = bf16[6144,1536]{1,0:T(8,128)(2,1)} fusion(bf16[1024,1536]{1,0:T(8,128)(2,1)} %fusion.24, f32[1024,6144]{1,0:T(8,128)} %fusion.42), kind=kOutput, calls=%fused_computation.10 | convolution fusion | flops 19393413120 | bytes 47185920 | tf_op jit(solution)/shard_map/dot_general | solution.py:319
  169.4 0.0 copy-done.1
  169.4 52.1 %fusion.7.up_ref = bf16[1536,6144]{1,0:T(8,128)(2,1)} fusion(bf16[1024,1536]{1,0:T(8,128)(2,1)S(1)} %copy-done.1, f32[1024,6144]{1,0:T(8,128)} %fusion.42, bf16[1024,1536]{1,0:T(8,128)(2,1)} %fusion.24, f32[1,6144,1536]{2,1,0:T(8,128)} %param.15), kind=kOutput, calls=%fused_computation.12 | convolution fusion | flops 38789971968 | bytes 88080384 | tf_op jit(solution)/shard_map/dot_general | solution.py:322
  221.5 367.3 %sum_gradients.1 = (bf16[1536,6144]{1,0:T(8,128)(2,1)}, bf16[6144,1536]{1,0:T(8,128)(2,1)}) custom-call(bf16[1536,6144]{1,0:T(8,128)(2,1)} %fusion.7.up_ref, bf16[6144,1536]{1,0:T(8,128)(2,1)} %convolution_convert_fusion.down_ref), custom_call_target="tpu_custom_call" | custom-call | flops 280000004096 | bytes 150994944 | tf_op jit(solution)/shard_map/sum_gradients/pallas_call | solution.py:191
  588.9 64.8 %second_up.1 = (f32[1536,6144]{1,0:T(8,128)}, f32[1536,6144]{1,0:T(8,128)}, bf16[1024,6144]{1,0:T(8,128)(2,1)}) custom-call(bf16[1024,1536]{1,0:T(8,128)(2,1)} %rows_ref.3, f32[1536,6144]{1,0:T(8,128)} %bitcast.57, f32[1536,6144]{1,0:T(8,128)} %bitcast.58, bf16[1536,6144]{1,0:T(8,128)(2,1)} %get-tuple-element.20.grad_ref), custom_call_target="tpu_custom_call" | custom-call | flops 19327352832 | bytes 150994944 | tf_op jit(solution)/shard_map/second_up/pallas_call | solution.py:253
  653.7 76.3 %second_down.1 = (f32[6144,1536]{1,0:T(8,128)}, f32[6144,1536]{1,0:T(8,128)}, f32[1024,1536]{1,0:T(8,128)}, bf16[1024,1536]{1,0:T(8,128)(2,1)}) custom-call(bf16[1024,1536]{1,0:T(8,128)(2,1)} %rows_ref.3, bf16[1024,6144]{1,0:T(8,128)(2,1)} %get-tuple-element.22.act_ref, f32[6144,1536]{1,0:T(8,128)} %bitcast.55, f32[6144,1536]{1,0:T(8,128)} %bitcast.56, ...), custom_call_target="tpu_custom_call" | custom-call | flops 19327352832 | bytes 150994944 | tf_op jit(solution)/shard_map/second_down/pallas_call | solution.py:253
  730.0 0.0 all-reduce.2.cloned.1.call-done.grad_ref
  730.0 47.5 %second_head.1 = (f32[1536,4096]{1,0:T(8,128)}, f32[1536,4096]{1,0:T(8,128)}, f32[1024,128]{1,0:T(8,128)}) custom-call(bf16[1024,1536]{1,0:T(8,128)(2,1)} %get-tuple-element.25.hidden_ref, bf16[1024,4096]{1,0:T(8,128)(2,1)} %target_ref.1, f32[1536,4096]{1,0:T(8,128)} %weight_ref.1, f32[1536,4096]{1,0:T(8,128)} %moment_ref.1, ...), custom_call_target="tpu_custom_call" | custom-call | flops 12884901888 | bytes 100663296 | tf_op jit(solution)/shard_map/second_head/pallas_call | solution.py:253
  777.5 1.2 reduce_sum.9
  778.8 0.6 broadcast_multiply_fusion
Async XLA Ops:
  7.2 33.3 %copy-start = (bf16[1024,1536]{1,0:T(8,128)(2,1)S(1)}, bf16[1024,1536]{1,0:T(8,128)(2,1)}, u32[]{:S(2)}) copy-start(bf16[1024,1536]{1,0:T(8,128)(2,1)} %param.10) | copy-start | bytes 9437188
  7.2 722.9 %all-reduce.2.cloned.1.call-start = ((), (), s32[]{:S(2)}) async-start(), calls=%async_computation | async-start | bytes 25165824 | tf_op jit(solution)/shard_map/psum | solution.py:316
  70.5 26.8 %copy-start.2 = (bf16[1024,1536]{1,0:T(8,128)(2,1)S(1)}, bf16[1024,1536]{1,0:T(8,128)(2,1)}, u32[]{:S(2)}) copy-start(bf16[1024,1536]{1,0:T(8,128)(2,1)} %add_convert_fusion) | copy-start | bytes 9437188
  138.0 31.4 %copy-start.1 = (bf16[1024,1536]{1,0:T(8,128)(2,1)S(1)}, bf16[1024,1536]{1,0:T(8,128)(2,1)}, u32[]{:S(2)}) copy-start(bf16[1024,1536]{1,0:T(8,128)(2,1)} %param.10) | copy-start | bytes 9437188
Sparse Core Ops, SparseCore 0:
  116.4 326.0 all-reduce.1

commit v2 on v1

--- a/solution.py
+++ b/solution.py
@@ -139,7 +139,7 @@
 PART_REFS = 2 + LEVELS + 1 + 4
 
 
-def sum_kernel(up_ref, down_ref, up_out, down_out, *scratch):
+def sum_kernel(up_ref, down_ref, later_ref, earlier_ref, up_out, down_out, later_out, *scratch):
     me = lax.axis_index('data')
     strides = (CORE, X, Y, Z_LOW, Z_HIGH)
     barrier = pltpu.get_barrier_semaphore()
@@ -183,25 +183,67 @@
     return shapes
 
 
-def sum_gradients(up_local, down_local):
+def sum_gradients(up_local, down_local, later, earlier):
     scratch = part_scratch(up_local.shape[0], CHUNK // 2, (1, 1, 0, 0, 0))
     scratch += part_scratch(CHUNK // 2, down_local.shape[1], (0, 0, 0, 0, 0))
     any_spec = pl.BlockSpec(memory_space=pl.ANY)
     size = up_local.size + down_local.size
     return pl.pallas_call(
         sum_kernel,
-        out_shape=[jax.ShapeDtypeStruct(up_local.shape, jnp.bfloat16), jax.ShapeDtypeStruct(down_local.shape, jnp.bfloat16)],
-        in_specs=[any_spec] * 2,
-        out_specs=[any_spec] * 2,
+        out_shape=[jax.ShapeDtypeStruct(array.shape, jnp.bfloat16) for array in (up_local, down_local, later)],
+        in_specs=[any_spec] * 4,
+        out_specs=[any_spec] * 3,
+        input_output_aliases={2: 2},
         scratch_shapes=scratch,
         compiler_params=pltpu.CompilerParams(collective_id=0, has_side_effects=True, vmem_limit_bytes=60 * 2**20),
         cost_estimate=pl.CostEstimate(flops=280 * 10**9, bytes_accessed=8 * size, transcendentals=0),
         name='sum_gradients',
-    )(up_local, down_local)
-
-
-def update(weight_ref, moment_ref, grad_ref, weight_out, moment_out, rate):
-    new_moment = MOMENTUM * moment_ref[...] + grad_ref[...].astype(jnp.float32)
+    )(up_local, down_local, later, earlier)
+
+
+def first_up_kernel(rows_ref, weight_ref, pre_out, act_out):
+    pre_act = jnp.dot(rows_ref[...], weight_ref[...].astype(jnp.bfloat16), preferred_element_type=jnp.float32)
+    pre_out[...] = pre_act
+    act_out[...] = jax.nn.gelu(pre_act).astype(jnp.bfloat16)
+
+
+def first_down_kernel(rows_ref, act_ref, weight_ref, top_out, hidden):
+    step = pl.program_id(0)
+
+    @pl.when(step == 0)
+    def _():
+        hidden[...] = rows_ref[...].astype(jnp.float32)
+
+    hidden[...] += jnp.dot(act_ref[...], weight_ref[...].astype(jnp.bfloat16), preferred_element_type=jnp.float32)
+
+    @pl.when(step == pl.num_programs(0) - 1)
+    def _():
+        top_out[...] = hidden[...].astype(jnp.bfloat16)
+
+
+def first_head_kernel(loss_scale, top_ref, target_ref, weight_ref, low_out, high_out, cotangent_out, cotangent):
+    step = pl.program_id(0)
+
+    @pl.when(step == 0)
+    def _():
+        cotangent[...] = jnp.zeros_like(cotangent)
+
+    weight_bf = weight_ref[...].astype(jnp.bfloat16)
+    logits = jnp.dot(top_ref[...], weight_bf, preferred_element_type=jnp.float32)
+    grad_logits = ((logits - target_ref[...].astype(jnp.float32)) * loss_scale).astype(jnp.bfloat16)
+    cotangent[...] += lax.dot_general(grad_logits, weight_bf, COL_DIMS, preferred_element_type=jnp.float32)
+    share = lax.dot_general(top_ref[...], grad_logits, ROW_DIMS, preferred_element_type=jnp.float32).astype(jnp.bfloat16)
+    low = low_out.shape[0]
+    low_out[...] = share[:low]
+    high_out[...] = share[low:]
+
+    @pl.when(step == pl.num_programs(0) - 1)
+    def _():
+        cotangent_out[...] = cotangent[...].astype(jnp.bfloat16)
+
+
+def update(weight_ref, moment_ref, grad, weight_out, moment_out, rate):
+    new_moment = MOMENTUM * moment_ref[...] + grad.astype(jnp.float32)
     new_weight = weight_ref[...] - rate * new_moment
     moment_out[...] = new_moment
     weight_out[...] = new_weight
@@ -209,14 +251,14 @@
 
 
 def up_kernel(rate, rows_ref, weight_ref, moment_ref, grad_ref, weight_out, moment_out, act_out):
-    weight_bf = update(weight_ref, moment_ref, grad_ref, weight_out, moment_out, rate)
+    weight_bf = update(weight_ref, moment_ref, grad_ref[...], weight_out, moment_out, rate)
     pre_act = jnp.dot(rows_ref[...], weight_bf, preferred_element_type=jnp.float32)
     act_out[...] = jax.nn.gelu(pre_act).astype(jnp.bfloat16)
 
 
 def down_kernel(rate, rows_ref, act_ref, weight_ref, moment_ref, grad_ref, weight_out, moment_out, hidden_out, hidden_bf_out):
     step = pl.program_id(0)
-    weight_bf = update(weight_ref, moment_ref, grad_ref, weight_out, moment_out, rate)
+    weight_bf = update(weight_ref, moment_ref, grad_ref[...], weight_out, moment_out, rate)
 
     @pl.when(step == 0)
     def _():
@@ -229,8 +271,9 @@
         hidden_bf_out[...] = hidden_out[...].astype(jnp.bfloat16)
 
 
-def head_kernel(rate, hidden_ref, target_ref, weight_ref, moment_ref, grad_ref, weight_out, moment_out, error_out):
-    weight_bf = update(weight_ref, moment_ref, grad_ref, weight_out, moment_out, rate)
+def head_kernel(rate, hidden_ref, target_ref, weight_ref, moment_ref, low_ref, high_ref, weight_out, moment_out, error_out):
+    grad = jnp.concatenate([low_ref[...], high_ref[...]], axis=0)
+    weight_bf = update(weight_ref, moment_ref, grad, weight_out, moment_out, rate)
     logits = jnp.dot(hidden_ref[...], weight_bf, preferred_element_type=jnp.float32)
     logit_err = logits - target_ref[...].astype(jnp.float32)
     squares = logit_err * logit_err
@@ -262,6 +305,54 @@
     )(*args)
 
 
+def low_rows(model):
+    return model * 5 // 12 // 16 * 16
+
+
+def first_call(kernel, steps, in_specs, out_specs, out_shape, scratch, flops, name, args):
+    return pl.pallas_call(
+        kernel,
+        grid=(steps,),
+        in_specs=in_specs,
+        out_specs=out_specs,
+        out_shape=out_shape,
+        scratch_shapes=scratch,
+        compiler_params=pltpu.CompilerParams(dimension_semantics=('arbitrary',), vmem_limit_bytes=60 * 2**20),
+        cost_estimate=pl.CostEstimate(flops=flops, bytes_accessed=4 * args[-1].size, transcendentals=0),
+        name=name,
+    )(*args)
+
+
+def first_up(rows, weight, tile=512):
+    tokens, (model, width) = rows.shape[0], weight.shape
+    cols = pl.BlockSpec((tokens, tile), lambda i: (0, i))
+    return first_call(
+        first_up_kernel, width // tile, [whole(rows.shape), pl.BlockSpec((model, tile), lambda i: (0, i))], [cols, cols],
+        [jax.ShapeDtypeStruct((tokens, width), jnp.float32), jax.ShapeDtypeStruct((tokens, width), jnp.bfloat16)],
+        [], 2 * tokens * model * width, 'first_up', (rows, weight))
+
+
+def first_down(rows, act, weight, tile=512):
+    tokens, (width, model) = rows.shape[0], weight.shape
+    return first_call(
+        first_down_kernel, width // tile,
+        [whole(rows.shape), pl.BlockSpec((tokens, tile), lambda i: (0, i)), pl.BlockSpec((tile, model), lambda i: (i, 0))],
+        whole(rows.shape), jax.ShapeDtypeStruct(rows.shape, jnp.bfloat16),
+        [pltpu.VMEM(rows.shape, jnp.float32)], 2 * tokens * model * width, 'first_down', (rows, act, weight))
+
+
+def first_head(top_bf, targets, weight, loss_scale, tile=512):
+    tokens, (model, width) = top_bf.shape[0], weight.shape
+    low = low_rows(model)
+    shares = [pl.BlockSpec((rows, tile), lambda i: (0, i)) for rows in (low, model - low)]
+    share_shapes = [jax.ShapeDtypeStruct((rows, width), jnp.bfloat16) for rows in (low, model - low)]
+    return first_call(
+        functools.partial(first_head_kernel, loss_scale), width // tile,
+        [whole(top_bf.shape), pl.BlockSpec((tokens, tile), lambda i: (0, i)), pl.BlockSpec((model, tile), lambda i: (0, i))],
+        [*shares, whole(top_bf.shape)], [*share_shapes, jax.ShapeDtypeStruct(top_bf.shape, jnp.bfloat16)],
+        [pltpu.VMEM(top_bf.shape, jnp.float32)], 6 * tokens * model * width, 'first_head', (top_bf, targets, weight))
+
+
 def second_up(rows, weight, moment, grad, rate, tile=256):
     tokens, (model, width) = rows.shape[0], weight.shape
     cols = pl.BlockSpec((model, tile), lambda i: (0, i))
@@ -273,7 +364,7 @@
         2 * tokens * model * width, 'second_up', (rows, weight, moment, grad))
 
 
-def second_down(rows, act, weight, moment, grad, rate, tile=256):
+def second_down(rows, act, weight, moment, grad, rate, tile=384):
     tokens, (width, model) = rows.shape[0], weight.shape
     band = pl.BlockSpec((tile, model), lambda i: (i, 0))
     return step_call(
@@ -284,15 +375,16 @@
         2 * tokens * model * width, 'second_down', (rows, act, weight, moment, grad))
 
 
-def second_head(hidden_bf, targets, weight, moment, grad, rate, tile=256):
+def second_head(hidden_bf, targets, weight, moment, low, high, rate, tile=256):
     tokens, (model, width) = hidden_bf.shape[0], weight.shape
     cols = pl.BlockSpec((model, tile), lambda i: (0, i))
+    shares = [pl.BlockSpec((low.shape[0], tile), lambda i: (0, i)), pl.BlockSpec((high.shape[0], tile), lambda i: (0, i))]
     return step_call(
         head_kernel, rate, width // tile,
-        [whole(hidden_bf.shape), pl.BlockSpec((tokens, tile), lambda i: (0, i)), cols, cols, cols],
+        [whole(hidden_bf.shape), pl.BlockSpec((tokens, tile), lambda i: (0, i)), cols, cols, *shares],
         [cols, cols, whole((tokens, 128))],
         [jax.ShapeDtypeStruct(weight.shape, jnp.float32)] * 2 + [jax.ShapeDtypeStruct((tokens, 128), jnp.float32)],
-        2 * tokens * model * width, 'second_head', (hidden_bf, targets, weight, moment, grad))
+        2 * tokens * model * width, 'second_head', (hidden_bf, targets, weight, moment, low, high))
 
 
 def solution(mesh):
@@ -302,29 +394,23 @@
         rate = RATE_BASE / w_up.shape[0]
         loss_scale = 1.0 / (inputs_now.shape[0] * data_size * w_head.shape[1])
         up, down, up_moment, down_moment = w_up[0], w_down[0], mom_up[0], mom_down[0]
-        up_bf, down_bf, head_bf = up.astype(jnp.bfloat16), down.astype(jnp.bfloat16), w_head.astype(jnp.bfloat16)
-
-        pre_act = jnp.dot(inputs_now, up_bf, preferred_element_type=jnp.float32)
-        act_f32, gelu_back = jax.vjp(jax.nn.gelu, pre_act)
-        act_bf = act_f32.astype(jnp.bfloat16)
-        hidden = inputs_now.astype(jnp.float32) + jnp.dot(act_bf, down_bf, preferred_element_type=jnp.float32)
-        top_bf = hidden.astype(jnp.bfloat16)
-        logits = jnp.dot(top_bf, head_bf, preferred_element_type=jnp.float32)
-        grad_logits = ((logits - targets_now.astype(jnp.float32)) * loss_scale).astype(jnp.bfloat16)
-
-        head_local = lax.dot_general(top_bf, grad_logits, ROW_DIMS, preferred_element_type=jnp.float32).astype(jnp.bfloat16)
-        grad_head = lax.psum(head_local, 'data')
-        grad_hidden = lax.dot_general(grad_logits, head_bf, COL_DIMS, preferred_element_type=jnp.float32)
-        grad_hidden_bf = grad_hidden.astype(jnp.bfloat16)
+        down_bf = down.astype(jnp.bfloat16)
+
+        pre_act, act_bf = first_up(inputs_now, up)
+        top_bf = first_down(inputs_now, act_bf, down)
+        low_local, high_local, grad_hidden_bf = first_head(top_bf, targets_now, w_head, loss_scale)
+        grad_low = lax.psum(low_local, 'data')
         down_local = lax.dot_general(act_bf, grad_hidden_bf, ROW_DIMS, preferred_element_type=jnp.float32).astype(jnp.bfloat16)
         grad_act = lax.dot_general(grad_hidden_bf, down_bf, COL_DIMS, preferred_element_type=jnp.float32)
+        gelu_back = jax.vjp(jax.nn.gelu, pre_act)[1]
         grad_pre = gelu_back(grad_act)[0].astype(jnp.bfloat16)
         up_local = lax.dot_general(inputs_now, grad_pre, ROW_DIMS, preferred_element_type=jnp.float32).astype(jnp.bfloat16)
-        grad_up, grad_down = sum_gradients(up_local, down_local)
+        grad_up, grad_down, high_local = sum_gradients(up_local, down_local, high_local, grad_low)
+        grad_high = lax.psum(high_local, 'data')
 
         up_new, up_moment_new, act_next = second_up(inputs_next, up, up_moment, grad_up, rate)
         down_new, down_moment_new, hidden_next, hidden_next_bf = second_down(inputs_next, act_next, down, down_moment, grad_down, rate)
-        head_new, head_moment_new, squares = second_head(hidden_next_bf, targets_next, w_head, mom_head, grad_head, rate)
+        head_new, head_moment_new, squares = second_head(hidden_next_bf, targets_next, w_head, mom_head, grad_low, grad_high, rate)
         errors = jnp.sum(squares, axis=-1) / (2.0 * w_head.shape[1])
         return (up_new[None], down_new[None], head_new, up_moment_new[None], down_moment_new[None], head_moment_new, errors, hidden_next)
 

time: 793 us -> 777 us (0.980)
  matrix products: 214 us -> 79.8 us
  waiting for transfers between devices: 0.04 us -> 95.5 us
  Pallas kernels: 556 us -> 585 us
    dot_general x5 -> x0, matrix products: 131 us -> none  [the longest x1 33.2 us: device_step(): pre_act = jnp.dot(inputs_now, up_bf, preferred_element_type=jnp.float32)]
    psum x1 -> x2, waiting for transfers between devices: 0.02 us -> 95.5 us  [the longest x1 70.4 us: device_step(): grad_low = lax.psum(low_local, 'data')]
    pallas_call x1 -> x4, Pallas kernels: 367 us -> 397 us  [the longest x1 285 us: sum_gradients(): pl.pallas_call(sum_kernel, out_shape=[jax.ShapeDtypeStruct(array.shape, j...]
  transfers between devices with their start and end apart: 1 -> 2, of which waited for: 0 -> 2; matrix products, arithmetic and copies ran while one was open for 13% -> 10% of each run, Pallas kernels for 65% -> 18%
where the time goes in v2:
time: 777 us
  Pallas kernels  585 us (75%)
  waiting for transfers between devices  95.5 us (12%)
  matrix products  79.8 us (10%)
  between operations  14.1 us (2%)
    pallas_call x1, Pallas kernels, sum_gradients(): pl.pallas_call(sum_kernel, out_shape=[jax.ShapeDtypeStruct(array.shape, j...  285 us
    pallas_call x3, Pallas kernels, step_call(): pl.pallas_call(functools.partial(kernel, rate), grid=(steps,), in_specs=i...  188 us
    pallas_call x3, Pallas kernels, first_call(): pl.pallas_call(kernel, grid=(steps,), in_specs=in_specs, out_specs=out_sp...  112 us
    psum x1, waiting for transfers between devices, device_step(): grad_low = lax.psum(low_local, 'data')  70.4 us
    dot_general x1, matrix products, device_step(): lax.dot_general(inputs_now, grad_pre, ROW_DIMS, preferred_element_type=jn...  51.9 us
    dot_general x1, matrix products, device_step(): lax.dot_general(act_bf, grad_hidden_bf, ROW_DIMS, preferred_element_type=...  27.9 us
    psum x1, waiting for transfers between devices, device_step(): grad_high = lax.psum(high_local, 'data')  25.1 us
  transfers between devices with their start and end apart: 2, of which 2 were waited for; matrix products, arithmetic and copies ran while one was open for 10% of the time, Pallas kernels for 18%

profile of v2, /device:TPU:0, one launch (start us, length us, event | category | flops | bytes accessed | tf_op | source)
XLA Modules:
  0.0 776.6 jit_solution(2384550464670161116)
XLA Ops:
  7.2 0.0 all-reduce.3.cloned.1.call-start
  7.2 35.1 %first_up.1 = (f32[1024,6144]{1,0:T(8,128)}, bf16[1024,6144]{1,0:T(8,128)(2,1)}) custom-call(bf16[1024,1536]{1,0:T(8,128)(2,1)} %rows_ref.5, f32[1536,6144]{1,0:T(8,128)} %bitcast.28), custom_call_target="tpu_custom_call" | custom-call | flops 19327352832 | bytes 37748736 | tf_op jit(solution)/shard_map/first_up/pallas_call | solution.py:313
  42.3 29.7 %first_down.1.top_ref = bf16[1024,1536]{1,0:T(8,128)(2,1)} custom-call(bf16[1024,1536]{1,0:T(8,128)(2,1)} %rows_ref.5, bf16[1024,6144]{1,0:T(8,128)(2,1)} %get-tuple-element.26.act_ref, f32[6144,1536]{1,0:T(8,128)} %bitcast.25), custom_call_target="tpu_custom_call" | custom-call | flops 19327352832 | bytes 37748736 | tf_op jit(solution)/shard_map/first_down/pallas_call | solution.py:313
  72.0 0.0 copy-start
  72.0 47.0 %first_head.1 = (bf16[640,4096]{1,0:T(8,128)(2,1)}, bf16[896,4096]{1,0:T(8,128)(2,1)}, bf16[1024,1536]{1,0:T(8,128)(2,1)}) custom-call(bf16[1024,1536]{1,0:T(8,128)(2,1)} %first_down.1.top_ref, bf16[1024,4096]{1,0:T(8,128)(2,1)} %target_ref.2, f32[1536,4096]{1,0:T(8,128)} %weight_ref.3), custom_call_target="tpu_custom_call" | custom-call | flops 38654705664 | bytes 25165824 | tf_op jit(solution)/shard_map/first_head/pallas_call | solution.py:313
  119.0 0.0 all-reduce.3.cloned.1.call-update
  119.0 0.2 all-reduce.5.cloned.1.call-start
  119.3 0.0 copy-done
  119.3 51.9 %fusion.7.up_ref = bf16[1536,6144]{1,0:T(8,128)(2,1)} fusion(bf16[1024,1536]{1,0:T(8,128)(2,1)S(1)} %copy-done, f32[1024,6144]{1,0:T(8,128)} %get-tuple-element.28, bf16[1024,1536]{1,0:T(8,128)(2,1)} %get-tuple-element.27, f32[1,6144,1536]{2,1,0:T(8,128)} %param.15), kind=kOutput, calls=%fused_computation.11 | convolution fusion | flops 38789971968 | bytes 88080384 | tf_op jit(solution)/shard_map/dot_general | solution.py:407
  171.1 27.9 %convolution_convert_fusion.down_ref = bf16[6144,1536]{1,0:T(8,128)(2,1)} fusion(bf16[1024,6144]{1,0:T(8,128)(2,1)} %get-tuple-element.26.act_ref, bf16[1024,1536]{1,0:T(8,128)(2,1)} %get-tuple-element.27), kind=kOutput, calls=%fused_computation.9 | convolution fusion | flops 19336790016 | bytes 34603008 | tf_op jit(solution)/shard_map/dot_general | solution.py:403
  199.0 70.4 %all-reduce.3.cloned.1.call-done.earlier_ref.low_ref = bf16[640,4096]{1,0:T(8,128)(2,1)} async-done(((bf16[640,4096]{1,0:T(8,128)(2,1)}), bf16[640,4096]{1,0:T(8,128)(2,1)}) %all-reduce.3.cloned.1.call-update) | async-done | bytes 5242896 | tf_op jit(solution)/shard_map/psum | solution.py:402
  269.4 285.5 %sum_gradients.1 = (bf16[1536,6144]{1,0:T(8,128)(2,1)}, bf16[6144,1536]{1,0:T(8,128)(2,1)}, bf16[896,4096]{1,0:T(8,128)(2,1)}) custom-call(bf16[1536,6144]{1,0:T(8,128)(2,1)} %fusion.7.up_ref, bf16[6144,1536]{1,0:T(8,128)(2,1)} %convolution_convert_fusion.down_ref, bf16[896,4096]{1,0:T(8,128)(2,1)} %get-tuple-element.29.later_ref, ...), custom_call_target="tpu_custom_call", output_to_operand_aliasing={{2}: (2, {})} | custom-call | flops 280000004096 | bytes 150994944 | tf_op jit(solution)/shard_map/sum_gradients/pallas_call | solution.py:191
  554.9 0.0 all-reduce.5.cloned.1.call-update
  554.9 64.8 %second_up.1 = (f32[1536,6144]{1,0:T(8,128)}, f32[1536,6144]{1,0:T(8,128)}, bf16[1024,6144]{1,0:T(8,128)(2,1)}) custom-call(bf16[1024,1536]{1,0:T(8,128)(2,1)} %rows_ref.7, f32[1536,6144]{1,0:T(8,128)} %bitcast.29, f32[1536,6144]{1,0:T(8,128)} %bitcast.30, bf16[1536,6144]{1,0:T(8,128)(2,1)} %get-tuple-element.31.grad_ref), custom_call_target="tpu_custom_call" | custom-call | flops 19327352832 | bytes 150994944 | tf_op jit(solution)/shard_map/second_up/pallas_call | solution.py:296
  619.7 75.7 %second_down.1 = (f32[6144,1536]{1,0:T(8,128)}, f32[6144,1536]{1,0:T(8,128)}, f32[1024,1536]{1,0:T(8,128)}, bf16[1024,1536]{1,0:T(8,128)(2,1)}) custom-call(bf16[1024,1536]{1,0:T(8,128)(2,1)} %rows_ref.7, bf16[1024,6144]{1,0:T(8,128)(2,1)} %get-tuple-element.33.act_ref, f32[6144,1536]{1,0:T(8,128)} %bitcast.26, f32[6144,1536]{1,0:T(8,128)} %bitcast.27, ...), custom_call_target="tpu_custom_call" | custom-call | flops 19327352832 | bytes 150994944 | tf_op jit(solution)/shard_map/second_down/pallas_call | solution.py:296
  695.4 25.1 %all-reduce.5.cloned.1.call-done.high_ref = bf16[896,4096]{1,0:T(8,128)(2,1)} async-done(((bf16[896,4096]{1,0:T(8,128)(2,1)}), bf16[896,4096]{1,0:T(8,128)(2,1)}) %all-reduce.5.cloned.1.call-update) | async-done | bytes 7340048 | tf_op jit(solution)/shard_map/psum | solution.py:409
  720.6 47.4 %second_head.1 = (f32[1536,4096]{1,0:T(8,128)}, f32[1536,4096]{1,0:T(8,128)}, f32[1024,128]{1,0:T(8,128)}) custom-call(bf16[1024,1536]{1,0:T(8,128)(2,1)} %get-tuple-element.36.hidden_ref, bf16[1024,4096]{1,0:T(8,128)(2,1)} %target_ref.3, f32[1536,4096]{1,0:T(8,128)} %weight_ref.3, f32[1536,4096]{1,0:T(8,128)} %moment_ref.1, ...), custom_call_target="tpu_custom_call" | custom-call | flops 12884901888 | bytes 58720256 | tf_op jit(solution)/shard_map/second_head/pallas_call | solution.py:296
  767.9 1.2 reduce_sum.9
  769.2 0.6 broadcast_multiply_fusion
Async XLA Ops:
  7.2 262.2 %all-reduce.3.cloned.1.call-start = ((), (), s32[]{:S(2)}) async-start(), calls=%async_computation | async-start | bytes 10485760 | tf_op jit(solution)/shard_map/psum | solution.py:402
  72.0 47.2 %copy-start = (bf16[1024,1536]{1,0:T(8,128)(2,1)S(1)}, bf16[1024,1536]{1,0:T(8,128)(2,1)}, u32[]{:S(2)}) copy-start(bf16[1024,1536]{1,0:T(8,128)(2,1)} %rows_ref.5) | copy-start | bytes 9437188
  119.0 601.5 %all-reduce.5.cloned.1.call-start = ((), (), s32[]{:S(2)}) async-start(), calls=%async_computation.1 | async-start | bytes 14680064 | tf_op jit(solution)/shard_map/psum | solution.py:409
Sparse Core Ops, SparseCore 0:
  119.2 150.1 all-reduce.2
  555.0 165.5 all-reduce.4

commit v3 on v2

--- a/solution.py
+++ b/solution.py
@@ -14,7 +14,7 @@
 MESH = pl.DeviceIdType.MESH
 
 CORE, X, Y, Z_LOW, Z_HIGH = 1, 2, 4, 8, 16
-CHUNK = 512
+CHUNK = 256
 ACC_SLOTS, RX_SLOTS, SUM_SLOTS = 6, 4, 8
 LEVELS = 4
 
@@ -28,11 +28,13 @@
 
 
 class Part:
-    def __init__(self, me, axis_chunk, order, axes, src, out, acc, rx, total, send_sem, recv_sem, load_sem, store_sem):
+    def __init__(self, me, axis_chunk, order, axes, src, out, span, first, acc, rx, total, send_sem, recv_sem, load_sem, store_sem):
         self.me, self.axis_chunk, self.order = me, axis_chunk, order
         self.src, self.out, self.acc, self.rx, self.total = src, out, acc, rx, total
         self.send_sem, self.recv_sem, self.load_sem, self.store_sem = send_sem, recv_sem, load_sem, store_sem
-        self.chunks = src.shape[axis_chunk] // CHUNK
+        self.base, self.chunks = span
+        self.first = first
+        self.acc_slots, self.rx_slots, self.sum_slots = acc.shape[0], rx[0].shape[0], total.shape[0]
         nr, nc = acc.shape[1], acc.shape[2]
         self.keep, self.send = [(0, 0, nr, nc)], [None]
         for level in range(1, LEVELS + 1):
@@ -49,7 +51,7 @@
 
     def half(self, ref, chunk, which):
         size = CHUNK // 2
-        start = pl.multiple_of(chunk * CHUNK + which * size, size)
+        start = pl.multiple_of((chunk + self.base) * CHUNK + which * size, size)
         if self.axis_chunk == 0:
             return ref.at[pl.ds(start, size), :]
         return ref.at[:, pl.ds(start, size)]
@@ -61,7 +63,7 @@
 
     def copy(self, phase, chunk):
         me = self.me
-        acc_slot, rx_slot, sum_slot = lax.rem(chunk, ACC_SLOTS), lax.rem(chunk, RX_SLOTS), lax.rem(chunk, SUM_SLOTS)
+        acc_slot, rx_slot, sum_slot = lax.rem(chunk, self.acc_slots), lax.rem(chunk, self.rx_slots), lax.rem(chunk, self.sum_slots)
         core = bit_of(me, CORE)
         if phase == 0:
             source, target = self.half(self.src, chunk, 1 - core), self.rx[0].at[rx_slot]
@@ -83,15 +85,15 @@
         )
 
     def load(self, chunk):
-        slot = lax.rem(chunk, ACC_SLOTS)
+        slot = lax.rem(chunk, self.acc_slots)
         return pltpu.make_async_copy(self.half(self.src, chunk, bit_of(self.me, CORE)), self.acc.at[slot], self.load_sem.at[slot])
 
     def store(self, chunk):
-        slot = lax.rem(chunk, SUM_SLOTS)
+        slot = lax.rem(chunk, self.sum_slots)
         return pltpu.make_async_copy(self.total.at[slot], self.half(self.out, chunk, bit_of(self.me, CORE)), self.store_sem.at[slot])
 
     def add(self, chunk, level, region, parent, target, target_slot):
-        acc_slot, rx_slot = lax.rem(chunk, ACC_SLOTS), lax.rem(chunk, RX_SLOTS)
+        acc_slot, rx_slot = lax.rem(chunk, self.acc_slots), lax.rem(chunk, self.rx_slots)
         r0, c0, nr, nc = region
         rel_r, rel_c = r0 - parent[0], c0 - parent[1]
         rows = max(16, min(nr, 24576 // nc))
@@ -118,14 +120,14 @@
             self.load(chunk).wait()
         self.copy(number - 1, chunk).wait()
         if number <= LEVELS:
-            slot = lax.rem(chunk, ACC_SLOTS)
+            slot = lax.rem(chunk, self.acc_slots)
             parent = self.keep[number - 1]
             self.add(chunk, number - 1, self.send[number], parent, self.acc, slot)
             self.copy(number, chunk).start()
             self.add(chunk, number - 1, self.keep[number], parent, self.acc, slot)
         elif number == LEVELS + 1:
             last = self.keep[LEVELS]
-            self.add(chunk, LEVELS, last, last, self.total, lax.rem(chunk, SUM_SLOTS))
+            self.add(chunk, LEVELS, last, last, self.total, lax.rem(chunk, self.sum_slots))
             self.copy(number, chunk).start()
         elif number <= 2 * LEVELS:
             self.copy(number, chunk).start()
@@ -137,9 +139,10 @@
 
 
 PART_REFS = 2 + LEVELS + 1 + 4
-
-
-def sum_kernel(up_ref, down_ref, later_ref, earlier_ref, up_out, down_out, later_out, *scratch):
+COL_AXES, ROW_AXES = (1, 0, 0, 0, 0), (0, 0, 0, 0, 1)
+
+
+def sum_kernel(up_ref, down_ref, head_ref, up_out, down_out, head_out, *scratch):
     me = lax.axis_index('data')
     strides = (CORE, X, Y, Z_LOW, Z_HIGH)
     barrier = pltpu.get_barrier_semaphore()
@@ -147,58 +150,67 @@
         pl.semaphore_signal(barrier, inc=1, device_id=(partner_of(me, stride),), device_id_type=MESH)
     pl.semaphore_wait(barrier, len(strides))
 
-    def build(axis_chunk, order, axes, src, out, refs):
+    def build(index, src, out, span, first):
+        refs = scratch[index * PART_REFS:(index + 1) * PART_REFS]
         acc, rx, total = refs[0], refs[1:2 + LEVELS], refs[2 + LEVELS]
-        return Part(me, axis_chunk, order, axes, src, out, acc, rx, total, *refs[3 + LEVELS:])
-
+        order = (CORE, X, Z_LOW, Y, Z_HIGH) if index % 2 == 0 else (CORE, Y, Z_LOW, X, Z_HIGH)
+        axis_chunk, axes = (0, ROW_AXES) if src is down_ref else (1, COL_AXES)
+        return Part(me, axis_chunk, order, axes, src, out, span, first, acc, rx, total, *refs[3 + LEVELS:])
+
+    head_half = head_ref.shape[1] // CHUNK // 2
     parts = (
-        build(1, (CORE, X, Z_LOW, Y, Z_HIGH), (1, 1, 0, 0, 0), up_ref, up_out, scratch[:PART_REFS]),
-        build(0, (CORE, Y, Z_LOW, X, Z_HIGH), (0, 0, 0, 0, 0), down_ref, down_out, scratch[PART_REFS:]),
+        build(2, head_ref, head_out, (0, head_half), 0),
+        build(3, head_ref, head_out, (head_half, head_half), 0),
+        build(0, up_ref, up_out, (0, up_ref.shape[1] // CHUNK), head_half),
+        build(1, down_ref, down_out, (0, down_ref.shape[0] // CHUNK), head_half),
     )
     stages = 2 * LEVELS + 3
 
     def tick(t, carry):
         for number in range(stages):
             for part in parts:
-                chunk = t - number
+                chunk = t - number - part.first
 
                 @pl.when(jnp.logical_and(chunk >= 0, chunk < part.chunks))
                 def _():
                     part.stage(number, chunk)
         return carry
 
-    lax.fori_loop(0, max(part.chunks for part in parts) + stages - 1, tick, 0)
-
-
-def part_scratch(rows, cols, axes):
-    shapes = [pltpu.VMEM((ACC_SLOTS, rows, cols), jnp.bfloat16), pltpu.VMEM((RX_SLOTS, rows, cols), jnp.bfloat16)]
+    lax.fori_loop(0, max(part.first + part.chunks for part in parts) + stages - 1, tick, 0)
+
+
+def part_scratch(rows, cols, axes, slots):
+    acc_slots, rx_slots, sum_slots = slots
+    shapes = [pltpu.VMEM((acc_slots, rows, cols), jnp.bfloat16), pltpu.VMEM((rx_slots, rows, cols), jnp.bfloat16)]
     nr, nc = rows, cols
     for level in range(1, LEVELS + 1):
         nr, nc = (nr // 2, nc) if axes[level] == 0 else (nr, nc // 2)
-        shapes.append(pltpu.VMEM((RX_SLOTS, nr, nc), jnp.bfloat16))
-    shapes.append(pltpu.VMEM((SUM_SLOTS, rows, cols), jnp.bfloat16))
+        shapes.append(pltpu.VMEM((rx_slots, nr, nc), jnp.bfloat16))
+    shapes.append(pltpu.VMEM((sum_slots, rows, cols), jnp.bfloat16))
     phases = 2 * LEVELS + 2
-    shapes += [pltpu.SemaphoreType.DMA((phases, RX_SLOTS)), pltpu.SemaphoreType.DMA((phases, RX_SLOTS))]
-    shapes += [pltpu.SemaphoreType.DMA((ACC_SLOTS,)), pltpu.SemaphoreType.DMA((SUM_SLOTS,))]
+    shapes += [pltpu.SemaphoreType.DMA((phases, rx_slots)), pltpu.SemaphoreType.DMA((phases, rx_slots))]
+    shapes += [pltpu.SemaphoreType.DMA((acc_slots,)), pltpu.SemaphoreType.DMA((sum_slots,))]
     return shapes
 
 
-def sum_gradients(up_local, down_local, later, earlier):
-    scratch = part_scratch(up_local.shape[0], CHUNK // 2, (1, 1, 0, 0, 0))
-    scratch += part_scratch(CHUNK // 2, down_local.shape[1], (0, 0, 0, 0, 0))
+def sum_gradients(up_local, down_local, head_local):
+    slots, head_slots = (ACC_SLOTS, RX_SLOTS, SUM_SLOTS), (head_local.shape[1] // CHUNK // 2,) * 3
+    model = up_local.shape[0]
+    scratch = part_scratch(model, CHUNK // 2, COL_AXES, slots) + part_scratch(CHUNK // 2, model, ROW_AXES, slots)
+    scratch += part_scratch(model, CHUNK // 2, COL_AXES, head_slots) * 2
     any_spec = pl.BlockSpec(memory_space=pl.ANY)
-    size = up_local.size + down_local.size
+    arrays = (up_local, down_local, head_local)
+    size = sum(array.size for array in arrays)
     return pl.pallas_call(
         sum_kernel,
-        out_shape=[jax.ShapeDtypeStruct(array.shape, jnp.bfloat16) for array in (up_local, down_local, later)],
-        in_specs=[any_spec] * 4,
+        out_shape=[jax.ShapeDtypeStruct(array.shape, jnp.bfloat16) for array in arrays],
+        in_specs=[any_spec] * 3,
         out_specs=[any_spec] * 3,
-        input_output_aliases={2: 2},
         scratch_shapes=scratch,
-        compiler_params=pltpu.CompilerParams(collective_id=0, has_side_effects=True, vmem_limit_bytes=60 * 2**20),
+        compiler_params=pltpu.CompilerParams(collective_id=0, has_side_effects=True, vmem_limit_bytes=62 * 2**20),
         cost_estimate=pl.CostEstimate(flops=280 * 10**9, bytes_accessed=8 * size, transcendentals=0),
         name='sum_gradients',
-    )(up_local, down_local, later, earlier)
+    )(*arrays)
 
 
 def first_up_kernel(rows_ref, weight_ref, pre_out, act_out):
@@ -221,7 +233,7 @@
         top_out[...] = hidden[...].astype(jnp.bfloat16)
 
 
-def first_head_kernel(loss_scale, top_ref, target_ref, weight_ref, low_out, high_out, cotangent_out, cotangent):
+def first_head_kernel(loss_scale, top_ref, target_ref, weight_ref, share_out, cotangent_out, cotangent):
     step = pl.program_id(0)
 
     @pl.when(step == 0)
@@ -232,10 +244,7 @@
     logits = jnp.dot(top_ref[...], weight_bf, preferred_element_type=jnp.float32)
     grad_logits = ((logits - target_ref[...].astype(jnp.float32)) * loss_scale).astype(jnp.bfloat16)
     cotangent[...] += lax.dot_general(grad_logits, weight_bf, COL_DIMS, preferred_element_type=jnp.float32)
-    share = lax.dot_general(top_ref[...], grad_logits, ROW_DIMS, preferred_element_type=jnp.float32).astype(jnp.bfloat16)
-    low = low_out.shape[0]
-    low_out[...] = share[:low]
-    high_out[...] = share[low:]
+    share_out[...] = lax.dot_general(top_ref[...], grad_logits, ROW_DIMS, preferred_element_type=jnp.float32).astype(jnp.bfloat16)
 
     @pl.when(step == pl.num_programs(0) - 1)
     def _():
@@ -271,9 +280,8 @@
         hidden_bf_out[...] = hidden_out[...].astype(jnp.bfloat16)
 
 
-def head_kernel(rate, hidden_ref, target_ref, weight_ref, moment_ref, low_ref, high_ref, weight_out, moment_out, error_out):
-    grad = jnp.concatenate([low_ref[...], high_ref[...]], axis=0)
-    weight_bf = update(weight_ref, moment_ref, grad, weight_out, moment_out, rate)
+def head_kernel(rate, hidden_ref, target_ref, weight_ref, moment_ref, grad_ref, weight_out, moment_out, error_out):
+    weight_bf = update(weight_ref, moment_ref, grad_ref[...], weight_out, moment_out, rate)
     logits = jnp.dot(hidden_ref[...], weight_bf, preferred_element_type=jnp.float32)
     logit_err = logits - target_ref[...].astype(jnp.float32)
     squares = logit_err * logit_err
@@ -303,10 +311,6 @@
         cost_estimate=pl.CostEstimate(flops=flops, bytes_accessed=16 * args[-1].size, transcendentals=0),
         name=name,
     )(*args)
-
-
-def low_rows(model):
-    return model * 5 // 12 // 16 * 16
 
 
 def first_call(kernel, steps, in_specs, out_specs, out_shape, scratch, flops, name, args):
@@ -343,13 +347,11 @@
 
 def first_head(top_bf, targets, weight, loss_scale, tile=512):
     tokens, (model, width) = top_bf.shape[0], weight.shape
-    low = low_rows(model)
-    shares = [pl.BlockSpec((rows, tile), lambda i: (0, i)) for rows in (low, model - low)]
-    share_shapes = [jax.ShapeDtypeStruct((rows, width), jnp.bfloat16) for rows in (low, model - low)]
+    cols = pl.BlockSpec((model, tile), lambda i: (0, i))
     return first_call(
         functools.partial(first_head_kernel, loss_scale), width // tile,
-        [whole(top_bf.shape), pl.BlockSpec((tokens, tile), lambda i: (0, i)), pl.BlockSpec((model, tile), lambda i: (0, i))],
-        [*shares, whole(top_bf.shape)], [*share_shapes, jax.ShapeDtypeStruct(top_bf.shape, jnp.bfloat16)],
+        [whole(top_bf.shape), pl.BlockSpec((tokens, tile), lambda i: (0, i)), cols],
+        [cols, whole(top_bf.shape)], [jax.ShapeDtypeStruct((model, width), jnp.bfloat16), jax.ShapeDtypeStruct(top_bf.shape, jnp.bfloat16)],
         [pltpu.VMEM(top_bf.shape, jnp.float32)], 6 * tokens * model * width, 'first_head', (top_bf, targets, weight))
 
 
@@ -375,16 +377,15 @@
         2 * tokens * model * width, 'second_down', (rows, act, weight, moment, grad))
 
 
-def second_head(hidden_bf, targets, weight, moment, low, high, rate, tile=256):
+def second_head(hidden_bf, targets, weight, moment, grad, rate, tile=256):
     tokens, (model, width) = hidden_bf.shape[0], weight.shape
     cols = pl.BlockSpec((model, tile), lambda i: (0, i))
-    shares = [pl.BlockSpec((low.shape[0], tile), lambda i: (0, i)), pl.BlockSpec((high.shape[0], tile), lambda i: (0, i))]
     return step_call(
         head_kernel, rate, width // tile,
-        [whole(hidden_bf.shape), pl.BlockSpec((tokens, tile), lambda i: (0, i)), cols, cols, *shares],
+        [whole(hidden_bf.shape), pl.BlockSpec((tokens, tile), lambda i: (0, i)), cols, cols, cols],
         [cols, cols, whole((tokens, 128))],
         [jax.ShapeDtypeStruct(weight.shape, jnp.float32)] * 2 + [jax.ShapeDtypeStruct((tokens, 128), jnp.float32)],
-        2 * tokens * model * width, 'second_head', (hidden_bf, targets, weight, moment, low, high))
+        2 * tokens * model * width, 'second_head', (hidden_bf, targets, weight, moment, grad))
 
 
 def solution(mesh):
@@ -398,19 +399,17 @@
 
         pre_act, act_bf = first_up(inputs_now, up)
         top_bf = first_down(inputs_now, act_bf, down)
-        low_local, high_local, grad_hidden_bf = first_head(top_bf, targets_now, w_head, loss_scale)
-        grad_low = lax.psum(low_local, 'data')
+        head_local, grad_hidden_bf = first_head(top_bf, targets_now, w_head, loss_scale)
         down_local = lax.dot_general(act_bf, grad_hidden_bf, ROW_DIMS, preferred_element_type=jnp.float32).astype(jnp.bfloat16)
         grad_act = lax.dot_general(grad_hidden_bf, down_bf, COL_DIMS, preferred_element_type=jnp.float32)
         gelu_back = jax.vjp(jax.nn.gelu, pre_act)[1]
         grad_pre = gelu_back(grad_act)[0].astype(jnp.bfloat16)
         up_local = lax.dot_general(inputs_now, grad_pre, ROW_DIMS, preferred_element_type=jnp.float32).astype(jnp.bfloat16)
-        grad_up, grad_down, high_local = sum_gradients(up_local, down_local, high_local, grad_low)
-        grad_high = lax.psum(high_local, 'data')
+        grad_up, grad_down, grad_head = sum_gradients(up_local, down_local, head_local)
 
         up_new, up_moment_new, act_next = second_up(inputs_next, up, up_moment, grad_up, rate)
         down_new, down_moment_new, hidden_next, hidden_next_bf = second_down(inputs_next, act_next, down, down_moment, grad_down, rate)
-        head_new, head_moment_new, squares = second_head(hidden_next_bf, targets_next, w_head, mom_head, grad_low, grad_high, rate)
+        head_new, head_moment_new, squares = second_head(hidden_next_bf, targets_next, w_head, mom_head, grad_head, rate)
         errors = jnp.sum(squares, axis=-1) / (2.0 * w_head.shape[1])
         return (up_new[None], down_new[None], head_new, up_moment_new[None], down_moment_new[None], head_moment_new, errors, hidden_next)
 

time: 777 us -> 752 us (0.968)
  waiting for transfers between devices: 95.5 us -> 0 us
  Pallas kernels: 585 us -> 669 us
  between operations: 14.1 us -> 0.66 us
    psum x2 -> x0, waiting for transfers between devices: 95.5 us -> none  [the longest x1 70.4 us: device_step(): grad_low = lax.psum(low_local, 'data')]
    pallas_call x1, Pallas kernels: 285 us -> 369 us  [sum_gradients(): pl.pallas_call(sum_kernel, out_shape=[jax.ShapeDtypeStruct(array.shape, j...]
  transfers between devices with their start and end apart: 2 -> 0, of which waited for: 2 -> 0; matrix products, arithmetic and copies ran while one was open for 10% -> 0% of each run, Pallas kernels for 18% -> 0%
where the time goes in v3:
time: 752 us; the launch traced here: 751 us
  Pallas kernels  669 us (89%)
  matrix products  79.9 us (11%)
    pallas_call x1, Pallas kernels, sum_gradients(): pl.pallas_call(sum_kernel, out_shape=[jax.ShapeDtypeStruct(array.shape, j...  369 us
    pallas_call x3, Pallas kernels, step_call(): pl.pallas_call(functools.partial(kernel, rate), grid=(steps,), in_specs=i...  188 us
    pallas_call x3, Pallas kernels, first_call(): pl.pallas_call(kernel, grid=(steps,), in_specs=in_specs, out_specs=out_sp...  112 us
    dot_general x1, matrix products, device_step(): lax.dot_general(inputs_now, grad_pre, ROW_DIMS, preferred_element_type=jn...  52 us
    dot_general x1, matrix products, device_step(): lax.dot_general(act_bf, grad_hidden_bf, ROW_DIMS, preferred_element_type=...  27.9 us

profile of v3, /device:TPU:0, one launch (start us, length us, event | category | flops | bytes accessed | tf_op | source)
XLA Modules:
  0.0 751.2 jit_solution(7953374051046514952)
XLA Ops:
  0.6 35.1 %first_up.1 = (f32[1024,6144]{1,0:T(8,128)}, bf16[1024,6144]{1,0:T(8,128)(2,1)}) custom-call(bf16[1024,1536]{1,0:T(8,128)(2,1)} %rows_ref.5, f32[1536,6144]{1,0:T(8,128)} %bitcast.28), custom_call_target="tpu_custom_call" | custom-call | flops 19327352832 | bytes 37748736 | tf_op jit(solution)/shard_map/first_up/pallas_call | solution.py:317
  35.8 29.7 %first_down.1.top_ref = bf16[1024,1536]{1,0:T(8,128)(2,1)} custom-call(bf16[1024,1536]{1,0:T(8,128)(2,1)} %rows_ref.5, bf16[1024,6144]{1,0:T(8,128)(2,1)} %get-tuple-element.25.act_ref, f32[6144,1536]{1,0:T(8,128)} %bitcast.25), custom_call_target="tpu_custom_call" | custom-call | flops 19327352832 | bytes 37748736 | tf_op jit(solution)/shard_map/first_down/pallas_call | solution.py:317
  65.5 0.0 copy-start
  65.5 46.9 %first_head.1 = (bf16[1536,4096]{1,0:T(8,128)(2,1)}, bf16[1024,1536]{1,0:T(8,128)(2,1)}) custom-call(bf16[1024,1536]{1,0:T(8,128)(2,1)} %first_down.1.top_ref, bf16[1024,4096]{1,0:T(8,128)(2,1)} %target_ref.2, f32[1536,4096]{1,0:T(8,128)} %weight_ref.3), custom_call_target="tpu_custom_call" | custom-call | flops 38654705664 | bytes 25165824 | tf_op jit(solution)/shard_map/first_head/pallas_call | solution.py:317
  112.4 0.0 copy-done
  112.4 52.0 %fusion.7.up_ref = bf16[1536,6144]{1,0:T(8,128)(2,1)} fusion(bf16[1024,1536]{1,0:T(8,128)(2,1)S(1)} %copy-done, f32[1024,6144]{1,0:T(8,128)} %get-tuple-element.27, bf16[1024,1536]{1,0:T(8,128)(2,1)} %get-tuple-element.26, f32[1,6144,1536]{2,1,0:T(8,128)} %param.15), kind=kOutput, calls=%fused_computation.11 | convolution fusion | flops 38789971968 | bytes 88080384 | tf_op jit(solution)/shard_map/dot_general | solution.py:407
  164.4 27.9 %convolution_convert_fusion.down_ref = bf16[6144,1536]{1,0:T(8,128)(2,1)} fusion(bf16[1024,6144]{1,0:T(8,128)(2,1)} %get-tuple-element.25.act_ref, bf16[1024,1536]{1,0:T(8,128)(2,1)} %get-tuple-element.26), kind=kOutput, calls=%fused_computation.9 | convolution fusion | flops 19336790016 | bytes 34603008 | tf_op jit(solution)/shard_map/dot_general | solution.py:403
  192.4 368.7 %sum_gradients.1 = (bf16[1536,6144]{1,0:T(8,128)(2,1)}, bf16[6144,1536]{1,0:T(8,128)(2,1)}, bf16[1536,4096]{1,0:T(8,128)(2,1)}) custom-call(bf16[1536,6144]{1,0:T(8,128)(2,1)} %fusion.7.up_ref, bf16[6144,1536]{1,0:T(8,128)(2,1)} %convolution_convert_fusion.down_ref, bf16[1536,4096]{1,0:T(8,128)(2,1)} %get-tuple-element.28.head_ref), custom_call_target="tpu_custom_call" | custom-call | flops 280000004096 | bytes 201326592 | tf_op jit(solution)/shard_map/sum_gradients/pallas_call | solution.py:204
  561.1 64.8 %second_up.1 = (f32[1536,6144]{1,0:T(8,128)}, f32[1536,6144]{1,0:T(8,128)}, bf16[1024,6144]{1,0:T(8,128)(2,1)}) custom-call(bf16[1024,1536]{1,0:T(8,128)(2,1)} %rows_ref.7, f32[1536,6144]{1,0:T(8,128)} %bitcast.29, f32[1536,6144]{1,0:T(8,128)} %bitcast.30, bf16[1536,6144]{1,0:T(8,128)(2,1)} %get-tuple-element.29.grad_ref), custom_call_target="tpu_custom_call" | custom-call | flops 19327352832 | bytes 150994944 | tf_op jit(solution)/shard_map/second_up/pallas_call | solution.py:304
  625.9 76.0 %second_down.1 = (f32[6144,1536]{1,0:T(8,128)}, f32[6144,1536]{1,0:T(8,128)}, f32[1024,1536]{1,0:T(8,128)}, bf16[1024,1536]{1,0:T(8,128)(2,1)}) custom-call(bf16[1024,1536]{1,0:T(8,128)(2,1)} %rows_ref.7, bf16[1024,6144]{1,0:T(8,128)(2,1)} %get-tuple-element.31.act_ref, f32[6144,1536]{1,0:T(8,128)} %bitcast.26, f32[6144,1536]{1,0:T(8,128)} %bitcast.27, ...), custom_call_target="tpu_custom_call" | custom-call | flops 19327352832 | bytes 150994944 | tf_op jit(solution)/shard_map/second_down/pallas_call | solution.py:304
  701.9 47.4 %second_head.1 = (f32[1536,4096]{1,0:T(8,128)}, f32[1536,4096]{1,0:T(8,128)}, f32[1024,128]{1,0:T(8,128)}) custom-call(bf16[1024,1536]{1,0:T(8,128)(2,1)} %get-tuple-element.34.hidden_ref, bf16[1024,4096]{1,0:T(8,128)(2,1)} %target_ref.3, f32[1536,4096]{1,0:T(8,128)} %weight_ref.3, f32[1536,4096]{1,0:T(8,128)} %moment_ref.1, ...), custom_call_target="tpu_custom_call" | custom-call | flops 12884901888 | bytes 100663296 | tf_op jit(solution)/shard_map/second_head/pallas_call | solution.py:304
  749.3 1.2 reduce_sum.9
  750.6 0.6 broadcast_multiply_fusion
Async XLA Ops:
  65.5 46.9 %copy-start = (bf16[1024,1536]{1,0:T(8,128)(2,1)S(1)}, bf16[1024,1536]{1,0:T(8,128)(2,1)}, u32[]{:S(2)}) copy-start(bf16[1024,1536]{1,0:T(8,128)(2,1)} %rows_ref.5) | copy-start | bytes 9437188
